TPU v7x, 512 devices: a whole 4x8x8 slice. The times are simulated.
512 devices in a mesh: row: 16 (over y_lo, z), col: 8 (over x, core), dp: 4 (over y_hi).
Axes of the slice: x: 4, y: 8 (y_hi: 4, y_lo: 2; y = y_hi * 2 + y_lo), z: 8, core: 2. Of those that a mesh axis runs over, the one named last changes fastest.
Arguments:
- tokens: bfloat16 [1536, 6144], P('dp', 'row'), parts along dimension 0, may hold values from -120 to 120
- norm_gain: float32 [6144], P('row'), may hold values from 0.25 to 1.75
- qkv_weight: bfloat16 [6144, 3, 3072], P('row', None, 'col'), may hold values from -2.5 to 2.5
- out_weight: bfloat16 [3072, 6144], P('col', 'row'), may hold values from -0.109375 to 0.109375
Outputs:
- projected: bfloat16 [1536, 6144], P('dp', 'row'), parts along dimension 0
There are 4 independent parts, one for each index of `dp`. A program takes and returns all parts, laid end to end along the dimension named above; an argument that names none is the same for every part. Nothing has to cross between parts.
All inputs are finite; a program needn't handle non-finite values.
Results may differ from a plain program's by a relative error of at most 0.025.
Values may be sent and summed in bfloat16 or wider, within the bound.
A program may use at most 64 MiB of HBM per device.

v0:
```python
import math

import jax
import jax.numpy as jnp
from jax import lax
from jax.sharding import PartitionSpec as P

K = 128


EPSILON = 1e-05


def copy_for_each(shard, axis):
    devices = lax.axis_size(axis)
    return lax.all_to_all(
        jnp.broadcast_to(shard[None], (devices, *shard.shape)), axis, 0, 0, tiled=True
    )


def over_copies(shard, axis):
    everything = copy_for_each(shard, axis)
    return jnp.sum(everything, axis=0)


def together(arrays, axis):
    ends = [0]
    for a in arrays:
        ends.append(ends[-1] + a.size)
    running = over_copies(jnp.concatenate([a.ravel() for a in arrays]), axis)
    return tuple((running[b:e].reshape(a.shape) for a, b, e in zip(arrays, ends, ends[1:])))


def filled_up(lines, devices):
    spare = -len(lines) % devices
    return jnp.pad(lines, [(0, spare)] + [(0, 0)] * (lines.ndim - 1))


def laid_out(parts, dim):
    lengths = list(parts.shape[1:])
    lengths[dim] *= parts.shape[0]
    return jnp.moveaxis(parts, 0, dim).reshape(lengths)


def gather_directly(shard, axis, dim):
    parts = copy_for_each(shard, axis)
    return laid_out(parts, dim)


def split_up(shard, dim, devices):
    lengths = shard.shape
    parts = shard.reshape(*lengths[:dim], devices, lengths[dim] // devices, *lengths[dim + 1 :])
    return jnp.moveaxis(parts, dim, 0)


def summed_on_arrival(shard, axis, dim):
    parts = split_up(shard, dim, lax.axis_size(axis))
    arrived = lax.all_to_all(parts, axis, split_axis=0, concat_axis=0, tiled=True)
    return arrived.astype(jnp.float32).sum(axis=0)


def nested_sum(shard, axes):
    lines = shard.reshape(-1, shard.shape[-1])
    padded = filled_up(lines, lax.axis_size(axes))
    whole = gather_directly(summed_on_arrival(padded, axes, 0).astype(jnp.bfloat16), axes, 0)
    return lax.slice_in_dim(whole, 0, len(lines)).reshape(shard.shape).astype(jnp.float32)


def over_copies_2(shard, axis):
    everything = copy_for_each(shard, axis)
    return jnp.sum(everything.astype(jnp.float32), axis=0)


def attend(queries, key_rows, value_rows):
    query_total = queries.shape[0]
    head_count = queries.shape[1] // K
    scaling = 1.0 / math.sqrt(K)
    split_keys = key_rows.reshape(key_rows.shape[0], head_count, K)
    split_values = value_rows.reshape(value_rows.shape[0], head_count, K)
    split_queries = queries.reshape(query_total, head_count, K)
    scores = (
        jnp.einsum("qhd,khd->hqk", split_queries, split_keys, preferred_element_type=jnp.float32)
        * scaling
    )
    largest = jnp.max(scores, axis=2, keepdims=True)
    exponent = jnp.exp(scores - largest)
    softmax_weights = (exponent / jnp.sum(exponent, axis=2, keepdims=True)).astype(jnp.bfloat16)
    mixed = jnp.einsum(
        "hqk,khd->qhd", softmax_weights, split_values, preferred_element_type=jnp.float32
    )
    result = mixed.astype(jnp.bfloat16)
    return result.reshape(query_total, head_count * K)


def shards(tokens, norm_gain, qkv_weight, out_weight):
    row_count, block_width = tokens.shape
    full_width = block_width * lax.axis_size("row")
    values = tokens.astype(jnp.float32)
    totals, squares = together(
        (jnp.sum(values, axis=1, keepdims=True), jnp.sum(values * values, axis=1, keepdims=True)),
        "row",
    )
    average = totals / full_width
    variance = squares / full_width - average * average
    centered = values - average
    normed = (centered * lax.rsqrt(variance + EPSILON) * norm_gain).astype(jnp.bfloat16)
    head_columns = qkv_weight.shape[2]
    partial_value = jnp.dot(
        normed,
        qkv_weight.reshape(block_width, 3 * head_columns),
        preferred_element_type=jnp.float32,
    )
    summed = (
        nested_sum(partial_value.astype(jnp.bfloat16), "row")
        .astype(jnp.bfloat16)
        .reshape(row_count, 3, head_columns)
    )
    attended = attend(summed[:, 0], summed[:, 1], summed[:, 2])
    partial_out = jnp.dot(attended, out_weight, preferred_element_type=jnp.float32)
    return (
        over_copies_2(partial_out.astype(jnp.bfloat16), "col")
        .astype(jnp.float32)
        .astype(jnp.bfloat16)
    )


def solution(mesh):
    in_specs = (P("dp", "row"), P("row"), P("row", None, "col"), P("col", "row"))
    out_specs = P("dp", "row")
    return jax.shard_map(shards, mesh=mesh, in_specs=in_specs, out_specs=out_specs, check_vma=False)
```

profile of v0, /device:TPU:57, one launch (start us, length us, event | category | flops | bytes accessed | tf_op | source)
XLA Modules:
  0.0 116.1 jit_solution(6283614068841369683)
XLA Ops:
  0.0 0.0 copy-start
  0.0 0.0 copy-start.1
  0.0 0.0 copy-start.2
  0.0 1.2 %convert_reduce_fusion = (f32[384]{0:T(512)S(1)}, f32[384]{0:T(512)S(1)}) fusion(bf16[384,384]{1,0:T(8,128)(2,1)} %param.4), kind=kLoop, calls=%fused_computation.11 | loop fusion | flops 589056 | bytes 297984 | tf_op jit(solution)/shard_map/reduce_sum | solution.py:100
  1.2 0.6 broadcast_in_dim.6
  1.9 11.2 %all-to-all-start = ((f32[16,1,768]{2,1,0:T(1,128)}), f32[16,1,768]{2,1,0:T(1,128)S(1)}, u32[]{:S(2)}, u32[]{:S(2)}) async-start(f32[16,1,768]{2,1,0:T(1,128)} %broadcast_in_dim.6), calls=%async_computation | async-start | bytes 98304 | tf_op jit(solution)/shard_map/all_to_all | solution.py:16
  13.1 2.5 %copy.21 = bf16[384,3,384]{0,2,1:T(8,128)(2,1)S(1)} copy(bf16[384,3,384]{2,0,1:T(8,128)(2,1)} %param.6) | data formatting | bytes 1769472 | tf_op args[2]
  15.6 3.8 %all-to-all-done = f32[16,1,768]{2,1,0:T(1,128)S(1)} async-done(((f32[16,1,768]{2,1,0:T(1,128)}), f32[16,1,768]{2,1,0:T(1,128)S(1)}, u32[]{:S(2)}, u32[]{:S(2)}) %all-to-all-start) | async-done | bytes 49184 | tf_op jit(solution)/shard_map/all_to_all | solution.py:16
  19.5 0.0 copy-done.1
  19.5 0.0 copy-done.2
  19.5 0.7 convolution_convert_fusion
  20.2 24.8 %all_to_all.21 = bf16[16,24,1152]{2,1,0:T(8,128)(2,1)S(1)} all-to-all(bf16[16,24,1152]{2,1,0:T(8,128)(2,1)S(1)} %bitcast.15), channel_id=1, replica_groups=mesh['row'=16,'col'=8,'dp'=4] {'row'}, dimensions={0} | all-to-all | bytes 1769472 | tf_op jit(solution)/shard_map/all_to_all | solution.py:58
  45.0 0.1 reduce_sum.63
  45.2 0.1 broadcast_in_dim.7
  45.2 29.4 %all_to_all.22 = bf16[16,24,1152]{2,1,0:T(8,128)(2,1)S(1)} all-to-all(bf16[16,24,1152]{2,1,0:T(8,128)(2,1)S(1)} %broadcast_in_dim.7), channel_id=1, replica_groups=mesh['row'=16,'col'=8,'dp'=4] {'row'}, dimensions={0} | all-to-all | bytes 1769472 | tf_op jit(solution)/shard_map/all_to_all | solution.py:16
  74.6 0.3 reshape.37
  74.9 1.2 %fusion.14 = (bf16[384,1,384]{2,1,0:T(2,128)(2,1)S(1)}, bf16[384,1,384]{2,1,0:T(2,128)(2,1)S(1)}, bf16[384,1,384]{2,1,0:T(2,128)(2,1)S(1)}) fusion(bf16[384,3,384]{2,1,0:T(4,128)(2,1)S(1)} %reshape.37), kind=kLoop, calls=%fused_computation.24 | loop fusion | bytes 1769472 | tf_op jit(solution)/shard_map/slice | solution.py:118
  76.1 0.9 copy.24
  77.0 0.9 copy.23
  77.9 0.9 copy.22
  78.7 0.8 fusion.15
  79.5 0.4 convolution_convert_fusion.2
  79.8 0.0 copy-done
  79.9 0.4 convolution_convert_fusion.1
  80.2 0.2 broadcast_in_dim.8
  80.4 34.5 %all_to_all.23 = bf16[8,384,384]{2,1,0:T(8,128)(2,1)S(1)} all-to-all(bf16[8,384,384]{2,1,0:T(8,128)(2,1)S(1)} %broadcast_in_dim.8), channel_id=1, replica_groups=mesh['row'=16,'col'=8,'dp'=4] {'col'}, dimensions={0} | all-to-all | bytes 4718592 | tf_op jit(solution)/shard_map/all_to_all | solution.py:16
  115.0 1.1 reduce_sum.65
  (3 shorter events, 0.1 us)
Async XLA Ops:
  0.0 79.8 %copy-start = (bf16[384,384]{1,0:T(8,128)(2,1)S(1)}, bf16[384,384]{1,0:T(8,128)(2,1)}, u32[]{:S(2)}) copy-start(bf16[384,384]{1,0:T(8,128)(2,1)} %param.7) | copy-start | bytes 884740
  0.0 19.5 %copy-start.1 = (bf16[384,384]{1,0:T(8,128)(2,1)S(1)}, bf16[384,384]{1,0:T(8,128)(2,1)}, u32[]{:S(2)}) copy-start(bf16[384,384]{1,0:T(8,128)(2,1)} %param.4) | copy-start | bytes 884740
  0.0 19.5 %copy-start.2 = (f32[384]{0:T(512)S(1)}, f32[384]{0:T(512)}, u32[]{:S(2)}) copy-start(f32[384]{0:T(512)} %param.5) | copy-start | bytes 4612
  1.9 17.5 %all-to-all-start = ((f32[16,1,768]{2,1,0:T(1,128)}), f32[16,1,768]{2,1,0:T(1,128)S(1)}, u32[]{:S(2)}, u32[]{:S(2)}) async-start(f32[16,1,768]{2,1,0:T(1,128)} %broadcast_in_dim.6), calls=%async_computation | async-start | bytes 98304 | tf_op jit(solution)/shard_map/all_to_all | solution.py:16
where the time goes:
time: 117 us; the launch traced here: 116 us
  blocking collectives  88.7 us (76%)
  starting transfers between devices  11.2 us (10%)
  local copies, waits for them, and re-layouts  7.49 us (6%)
  waiting for transfers between devices  3.82 us (3%)
  other arithmetic  2.5 us (2%)
  matrix products  2.2 us (2%)
    all_to_all x2, blocking collectives, copy_for_each(): lax.all_to_all(jnp.broadcast_to(shard[None], (devices, *shard.shape)), ax...  63.9 us
    all_to_all x1, blocking collectives, summed_on_arrival(): lax.all_to_all(parts, axis, split_axis=0, concat_axis=0, tiled=True)  24.8 us
    all_to_all x1, starting transfers between devices, copy_for_each(): lax.all_to_all(jnp.broadcast_to(shard[None], (devices, *shard.shape)), ax...  11.2 us
    all_to_all x1, waiting for transfers between devices, copy_for_each(): lax.all_to_all(jnp.broadcast_to(shard[None], (devices, *shard.shape)), ax...  3.82 us
    slice x4, local copies, waits for them, and re-layouts, shards(): attended = attend(summed[:, 0], summed[:, 1], summed[:, 2])  3.81 us
    unnamed x7, local copies, waits for them, and re-layouts  2.49 us
  transfers between devices with their start and end apart: 1, of which 1 were waited for; matrix products, arithmetic and copies ran while one was open for 2% of the time, Pallas kernels for 0%

commit v1 on v0

v1 whole, which is shorter than its diff:
```python
import math

import jax
import jax.numpy as jnp
from jax import lax
from jax.experimental import pallas as pl
from jax.experimental.pallas import tpu as pltpu
from jax.sharding import PartitionSpec as P

K = 128
EPSILON = 1e-05
F32 = jnp.float32
BF16 = jnp.bfloat16
T = 384
HALF = 192
BLOCK = 48
ZS = 8
COLS = 8
FEATURES = 6144
ORDER = (1, 2, 0)
MESH = pl.DeviceIdType.MESH


def owner_z(owner):
    return owner + owner // 2


def kernel(
    x_hbm, gain_ref, w_hbm, wo_hbm, o_ref,
    x_v, w_v, wo_v, lhs, aux_own, aux_all, part, y_buf, z_buf, z_in, acc, qkv, tall, att, p_buf, p_in,
    load_sem, aux_sems, auxz_send, auxz_recv, y_send, y_recv, z_send, z_recv,
    kv_send, kv_recv, at_send, at_recv, ay_send, ay_recv, rs_send, rs_recv, ag_send, ag_recv,
):
    row = lax.axis_index("row")
    col = lax.axis_index("col")
    y = row // ZS
    z = row % ZS
    active = y == col % 2
    partner = {"row": (1 - y) * ZS + z}
    is_owner = jnp.logical_and(active, z % 3 != 2)
    mine = z - (z + 1) // 3
    head = mine // 2
    half = mine % 2

    def at_z(other):
        return {"row": y * ZS + other}

    def remote(src, dst, send, recv, device):
        return pltpu.make_async_remote_copy(
            src_ref=src, dst_ref=dst, send_sem=send, recv_sem=recv, device_id=device, device_id_type=MESH
        )

    x_load = pltpu.make_async_copy(x_hbm, x_v, load_sem.at[0])
    x_load.start()
    w_loads = [pltpu.make_async_copy(w_hbm.at[j], w_v.at[j], load_sem.at[1 + j]) for j in range(3)]
    for j in ORDER:
        w_loads[j].start()
    wo_load = pltpu.make_async_copy(wo_hbm, wo_v, load_sem.at[4])
    wo_load.start()

    barrier = pltpu.get_barrier_semaphore()
    pl.semaphore_signal(barrier, inc=1, device_id=partner, device_id_type=MESH)
    for d in range(1, ZS):
        pl.semaphore_signal(barrier, inc=1, device_id=at_z((z + d) % ZS), device_id_type=MESH)
    for d in range(1, COLS):
        pl.semaphore_signal(barrier, inc=1, device_id={"col": (col + d) % COLS}, device_id_type=MESH)

    x_load.wait()
    values = x_v[...].astype(F32)
    mean = jnp.sum(values, axis=1, keepdims=True) * (1.0 / T)
    centered = values - mean
    squares = jnp.sum(centered * centered, axis=1, keepdims=True)
    gain = gain_ref[...].reshape(1, T)
    lhs[0:T, :] = (centered * gain).astype(BF16)
    high = gain.astype(BF16).astype(F32)
    rows = lax.broadcasted_iota(jnp.int32, (16, T), 0)
    lhs[T : T + 16, :] = jnp.where(rows == 0, high, jnp.where(rows == 1, gain - high, 0.0)).astype(BF16)
    lanes = lax.broadcasted_iota(jnp.int32, (T, 128), 1)
    turned = jnp.where(lanes == 0, mean, jnp.where(lanes == 1, squares, 0.0)).T
    aux_own[0:8, :] = turned[0:8, :]

    y_copies = [
        remote(y_buf.at[u], y_buf.at[u], y_send.at[u], y_recv.at[u], partner) for u in range(9)
    ]
    aux_copy = remote(aux_own, aux_all.at[z, 1], aux_sems.at[0], aux_sems.at[1], partner)

    for step, j in enumerate(ORDER):
        w_loads[j].wait()
        product = jnp.dot(lhs[...], w_v[j], preferred_element_type=F32)
        aux_own[2 + j : 3 + j, :] = product[T : T + 1, :] + product[T + 1 : T + 2, :]

        @pl.when(active)
        def _():
            for h in range(3):
                part[3 * j + h] = product[0:T, h * K : (h + 1) * K]

        @pl.when(jnp.logical_not(active))
        def _():
            for h in range(3):
                y_buf[3 * j + h] = product[0:T, h * K : (h + 1) * K].astype(BF16)

        if step == 0:
            pl.semaphore_wait(barrier, 1 + (ZS - 1) + (COLS - 1))

        @pl.when(jnp.logical_not(active))
        def _():
            for h in range(3):
                y_copies[3 * j + h].start()

    @pl.when(jnp.logical_not(active))
    def _():
        aux_copy.start()

    def z_copy(u, o):
        return remote(
            z_buf.at[u, o % 2], z_in.at[z, u // 3], z_send.at[u, o % 2], z_recv.at[z, u // 3], at_z(owner_z(o))
        )

    def aux_z_copy(o):
        return remote(aux_all.at[z], aux_all.at[z], auxz_send.at[o], auxz_recv.at[z], at_z(owner_z(o)))

    @pl.when(active)
    def _():
        aux_all[z, 0] = aux_own[...]
        aux_copy.wait_recv()
        for o in range(6):
            @pl.when(z != owner_z(o))
            def _(o=o):
                aux_z_copy(o).start()

        for j in ORDER:
            for h in range(3):
                u = 3 * j + h
                y_copies[u].wait_recv()
                for s in range(2):
                    o = 2 * h + s
                    tokens = slice(s * HALF, (s + 1) * HALF)
                    total = part[u, tokens, :] + y_buf[u, tokens, :].astype(F32)

                    @pl.when(z != owner_z(o))
                    def _(o=o, u=u, s=s, total=total):
                        z_buf[u, s] = total.astype(BF16)
                        z_copy(u, o).start()

                    @pl.when(z == owner_z(o))
                    def _(j=j, total=total):
                        acc[j] = total

    kv_copy = remote(
        qkv.at[pl.ds(1, 2), half], qkv.at[pl.ds(1, 2), half], kv_send.at[0], kv_recv.at[0], at_z(z + 1 - 2 * half)
    )

    def at_copy(o, d):
        return remote(att.at[o], att.at[o], at_send.at[d - 1], at_recv.at[o], at_z((z + d) % ZS))

    def ay_copy(o):
        return remote(att.at[o], att.at[o], ay_send.at[o], ay_recv.at[o], partner)

    @pl.when(is_owner)
    def _():
        for d in range(1, ZS):
            other = (z + d) % ZS
            remote(
                aux_all.at[other], aux_all.at[other], auxz_send.at[0], auxz_recv.at[other], at_z(other)
            ).wait_recv()
        flat = aux_all[...].reshape(2 * ZS, 8, T)
        means = flat[:, 0, :]
        average = jnp.sum(means, axis=0, keepdims=True) * (1.0 / 16)
        offsets = means - average
        spread = jnp.sum(flat[:, 1, :] + T * (offsets * offsets), axis=0, keepdims=True) * (1.0 / FEATURES)
        scale = lax.rsqrt(spread + EPSILON)
        stacked = jnp.concatenate([offsets, jnp.broadcast_to(scale, (112, T))], axis=0)
        tall[...] = stacked.T
        tall_half = tall[pl.ds(pl.multiple_of(half * HALF, HALF), HALF), :]
        scale_col = tall_half[:, 16:17]
        offset_cols = tall_half[:, 0:16]
        lane0 = pl.multiple_of(head * K, K)

        for j in ORDER:
            weights_sum = aux_all[:, :, 2 + j, pl.ds(lane0, K)].reshape(2 * ZS, K)
            total = acc[j] + jnp.dot(
                offset_cols, weights_sum, preferred_element_type=F32, precision=lax.Precision.HIGHEST
            )
            for d in range(1, ZS):
                other = (z + d) % ZS
                remote(
                    z_in.at[other, j], z_in.at[other, j], z_send.at[0, 0], z_recv.at[other, j], at_z(other)
                ).wait_recv()
                total = total + z_in[other, j].astype(F32)
            qkv[j, half] = (total * scale_col).astype(BF16)
            if j == 2:
                kv_copy.start()

        kv_copy.wait_recv()
        queries = qkv[0, half]
        keys = qkv[1].reshape(T, K)
        scores = lax.dot_general(
            queries, keys, (((1,), (1,)), ((), ())), preferred_element_type=F32
        ) * (1.0 / math.sqrt(K))
        exponent = jnp.exp(scores - jnp.max(scores, axis=1, keepdims=True))
        weights = (exponent / jnp.sum(exponent, axis=1, keepdims=True)).astype(BF16)
        mixed = jnp.dot(weights, qkv[2].reshape(T, K), preferred_element_type=F32)
        att[mine] = mixed.astype(BF16)
        for d in range(1, ZS):
            at_copy(mine, d).start()

    @pl.when(active)
    def _():
        for o in range(6):
            @pl.when(z != owner_z(o))
            def _(o=o):
                at_copy(o, 1).wait_recv()
            ay_copy(o).start()

    wo_load.wait()

    @pl.when(jnp.logical_not(active))
    def _():
        for o in range(6):
            ay_copy(o).wait_recv()

    for s in range(2):
        attended = jnp.concatenate([att[2 * h + s] for h in range(3)], axis=1)
        product = jnp.dot(attended, wo_v[...], preferred_element_type=F32).astype(BF16)
        for b in range(4):
            p_buf[4 * s + b] = product[b * BLOCK : (b + 1) * BLOCK, :]

    def rs_copy(d):
        other = (col + d) % COLS
        return remote(p_buf.at[other], p_in.at[col], rs_send.at[d - 1], rs_recv.at[col], {"col": other})

    def rs_arrival(d):
        other = (col + d) % COLS
        return remote(p_buf.at[col], p_in.at[other], rs_send.at[d - 1], rs_recv.at[other], {"col": other})

    my_rows = o_ref.at[pl.ds(pl.multiple_of(col * BLOCK, BLOCK), BLOCK), :]

    def ag_copy(d):
        other = (col + d) % COLS
        return remote(my_rows, my_rows, ag_send.at[d - 1], ag_recv.at[col], {"col": other})

    def ag_arrival(d):
        other = (col + d) % COLS
        rows_there = o_ref.at[pl.ds(pl.multiple_of(other * BLOCK, BLOCK), BLOCK), :]
        return remote(rows_there, rows_there, ag_send.at[d - 1], ag_recv.at[other], {"col": other})

    for d in range(1, COLS):
        rs_copy(d).start()
    total = p_buf[col].astype(F32)
    for d in range(1, COLS):
        rs_arrival(d).wait_recv()
        total = total + p_in[(col + d) % COLS].astype(F32)
    my_rows[...] = total.astype(BF16)
    for d in range(1, COLS):
        ag_copy(d).start()

    @pl.when(jnp.logical_not(active))
    def _():
        aux_copy.wait_send()
        for u in range(9):
            y_copies[u].wait_send()

    @pl.when(active)
    def _():
        for o in range(6):
            ay_copy(o).wait_send()

            @pl.when(z != owner_z(o))
            def _(o=o):
                aux_z_copy(o).wait_send()
                for j in range(3):
                    z_copy(3 * j + o // 2, o).wait_send()

    @pl.when(is_owner)
    def _():
        kv_copy.wait_send()
        for d in range(1, ZS):
            at_copy(mine, d).wait_send()

    for d in range(1, COLS):
        rs_copy(d).wait_send()
        ag_arrival(d).wait_recv()
    for d in range(1, COLS):
        ag_copy(d).wait_send()


def shards(tokens, norm_gain, qkv_weight, out_weight):
    dma = pltpu.SemaphoreType.DMA
    return pl.pallas_call(
        kernel,
        out_shape=jax.ShapeDtypeStruct((T, T), BF16),
        in_specs=[
            pl.BlockSpec(memory_space=pl.ANY),
            pl.BlockSpec(memory_space=pltpu.VMEM),
            pl.BlockSpec(memory_space=pl.ANY),
            pl.BlockSpec(memory_space=pl.ANY),
        ],
        out_specs=pl.BlockSpec(memory_space=pltpu.VMEM),
        scratch_shapes=[
            pltpu.VMEM((T, T), BF16),
            pltpu.VMEM((3, T, T), BF16),
            pltpu.VMEM((T, T), BF16),
            pltpu.VMEM((T + 16, T), BF16),
            pltpu.VMEM((8, T), F32),
            pltpu.VMEM((ZS, 2, 8, T), F32),
            pltpu.VMEM((9, T, K), F32),
            pltpu.VMEM((9, T, K), BF16),
            pltpu.VMEM((9, 2, HALF, K), BF16),
            pltpu.VMEM((ZS, 3, HALF, K), BF16),
            pltpu.VMEM((3, HALF, K), F32),
            pltpu.VMEM((3, 2, HALF, K), BF16),
            pltpu.VMEM((T, 128), F32),
            pltpu.VMEM((6, HALF, K), BF16),
            pltpu.VMEM((COLS, BLOCK, T), BF16),
            pltpu.VMEM((COLS, BLOCK, T), BF16),
            dma((5,)),
            dma((2,)),
            dma((6,)),
            dma((ZS,)),
            dma((9,)),
            dma((9,)),
            dma((9, 2)),
            dma((ZS, 3)),
            dma((1,)),
            dma((1,)),
            dma((ZS - 1,)),
            dma((6,)),
            dma((6,)),
            dma((6,)),
            dma((COLS - 1,)),
            dma((COLS,)),
            dma((COLS - 1,)),
            dma((COLS,)),
        ],
        compiler_params=pltpu.CompilerParams(collective_id=0, has_side_effects=True),
        name="sublayer",
    )(tokens, norm_gain, jnp.transpose(qkv_weight, (1, 0, 2)), out_weight)


def solution(mesh):
    in_specs = (P("dp", "row"), P("row"), P("row", None, "col"), P("col", "row"))
    out_specs = P("dp", "row")
    return jax.shard_map(shards, mesh=mesh, in_specs=in_specs, out_specs=out_specs, check_vma=False)
```

time: 117 us -> 68.7 us (0.59)
  blocking collectives: 88.7 us -> 0 us
  Pallas kernels: 0 us -> 66.8 us
  starting transfers between devices: 11.2 us -> 0 us
  local copies, waits for them, and re-layouts: 7.49 us -> 1.71 us
  waiting for transfers between devices: 3.82 us -> 0 us
  other arithmetic: 2.5 us -> 0 us
  matrix products: 2.2 us -> 0 us
    all_to_all x3 -> x0, blocking collectives: 88.7 us -> none  [the longest x2 63.9 us: copy_for_each(): lax.all_to_all(jnp.broadcast_to(shard[None], (devices, *shard.shape)), ax...]
    pallas_call x0 -> x1, Pallas kernels: none -> 66.8 us  [shards(): pl.pallas_call(kernel, out_shape=jax.ShapeDtypeStruct((T, T), BF16), in_s...]
    all_to_all x1 -> x0, starting transfers between devices: 11.2 us -> none  [copy_for_each(): lax.all_to_all(jnp.broadcast_to(shard[None], (devices, *shard.shape)), ax...]
    all_to_all x1 -> x0, waiting for transfers between devices: 3.82 us -> none  [copy_for_each(): lax.all_to_all(jnp.broadcast_to(shard[None], (devices, *shard.shape)), ax...]
    slice x4 -> x0, local copies, waits for them, and re-layouts: 3.81 us -> none  [shards(): attended = attend(summed[:, 0], summed[:, 1], summed[:, 2])]
    reduce_sum x4 -> x0, other arithmetic: 2.48 us -> none  [the longest x1 1.21 us: shards(): jnp.sum(values, axis=1, keepdims=True)]
    dot_general x3 -> x0, matrix products: 1.44 us -> none  [the longest x1 0.72 us: shards(): jnp.dot(normed, qkv_weight.reshape(block_width, 3 * head_columns), prefer...]
    unnamed x7 -> x1, local copies, waits for them, and re-layouts: 2.49 us -> 1.71 us
  transfers between devices with their start and end apart: 1 -> 0, of which waited for: 1 -> 0; matrix products, arithmetic and copies ran while one was open for 2% -> 0% of each run, Pallas kernels for 0% -> 0%
where the time goes in v1:
time: 68.7 us; the launch traced here: 68.5 us
  Pallas kernels  66.8 us (97%)
  local copies, waits for them, and re-layouts  1.71 us (2%)
    pallas_call x1, Pallas kernels, shards(): pl.pallas_call(kernel, out_shape=jax.ShapeDtypeStruct((T, T), BF16), in_s...  66.8 us
    unnamed x1, local copies, waits for them, and re-layouts  1.71 us

profile of v1, /device:TPU:57, one launch (start us, length us, event | category | flops | bytes accessed | tf_op | source)
XLA Modules:
  0.0 68.5 jit_solution(3658831673732177645)
XLA Ops:
  0.0 66.8 %sublayer.1 = bf16[384,384]{1,0:T(8,128)(2,1)} custom-call(bf16[384,384]{1,0:T(8,128)(2,1)} %x_hbm.1, f32[384]{0:T(512)} %gain_ref.1, bf16[3,384,384]{2,1,0:T(8,128)(2,1)} %bitcast.1, bf16[384,384]{1,0:T(8,128)(2,1)} %wo_hbm.1), custom_call_target="tpu_custom_call" | custom-call | tf_op jit(solution)/shard_map/sublayer/pallas_call | solution.py:289
  66.8 1.7 %copy.6 = bf16[384,384]{1,0:T(8,128)(2,1)} copy(bf16[384,384]{1,0:T(8,128)(2,1)} %sublayer.1) | data formatting | bytes 589824

commit v2 on v1

--- a/solution.py
+++ b/solution.py
@@ -22,12 +22,12 @@
 
 
 def owner_z(owner):
-    return owner + owner // 2
+    return owner + owner // 3
 
 
 def kernel(
-    x_hbm, gain_ref, w_hbm, wo_hbm, o_ref,
-    x_v, w_v, wo_v, lhs, aux_own, aux_all, part, y_buf, z_buf, z_in, acc, qkv, tall, att, p_buf, p_in,
+    x_hbm, gain_hbm, w_hbm, wo_hbm, o_ref,
+    x_v, gain_v, w_v, wo_v, lhs, aux_own, aux_all, part, y_buf, z_buf, z_in, acc, qkv, att, p_buf, p_in,
     load_sem, aux_sems, auxz_send, auxz_recv, y_send, y_recv, z_send, z_recv,
     kv_send, kv_recv, at_send, at_recv, ay_send, ay_recv, rs_send, rs_recv, ag_send, ag_recv,
 ):
@@ -37,8 +37,8 @@
     z = row % ZS
     active = y == col % 2
     partner = {"row": (1 - y) * ZS + z}
-    is_owner = jnp.logical_and(active, z % 3 != 2)
-    mine = z - (z + 1) // 3
+    is_owner = jnp.logical_and(active, z % 4 != 3)
+    mine = z - z // 4
     head = mine // 2
     half = mine % 2
 
@@ -55,6 +55,8 @@
     w_loads = [pltpu.make_async_copy(w_hbm.at[j], w_v.at[j], load_sem.at[1 + j]) for j in range(3)]
     for j in ORDER:
         w_loads[j].start()
+    gain_load = pltpu.make_async_copy(gain_hbm, gain_v, load_sem.at[5])
+    gain_load.start()
     wo_load = pltpu.make_async_copy(wo_hbm, wo_v, load_sem.at[4])
     wo_load.start()
 
@@ -70,24 +72,33 @@
     mean = jnp.sum(values, axis=1, keepdims=True) * (1.0 / T)
     centered = values - mean
     squares = jnp.sum(centered * centered, axis=1, keepdims=True)
-    gain = gain_ref[...].reshape(1, T)
+    gain_load.wait()
+    gain = gain_v[...].reshape(1, T)
     lhs[0:T, :] = (centered * gain).astype(BF16)
     high = gain.astype(BF16).astype(F32)
     rows = lax.broadcasted_iota(jnp.int32, (16, T), 0)
     lhs[T : T + 16, :] = jnp.where(rows == 0, high, jnp.where(rows == 1, gain - high, 0.0)).astype(BF16)
     lanes = lax.broadcasted_iota(jnp.int32, (T, 128), 1)
     turned = jnp.where(lanes == 0, mean, jnp.where(lanes == 1, squares, 0.0)).T
-    aux_own[0:8, :] = turned[0:8, :]
+    early = turned[0:8, :]
+    late = pltpu.roll(early, T - HALF, 1)
+    for o in range(6):
+        source = early if o % 2 == 0 else late
+        for r in range(2):
+            aux_own[0, o, 3 + 2 * r : 4 + 2 * r, :] = source[r : r + 1, 0:K]
+            aux_own[0, o, 4 + 2 * r : 5 + 2 * r, :] = source[r : r + 1, K : 2 * K]
 
     y_copies = [
         remote(y_buf.at[u], y_buf.at[u], y_send.at[u], y_recv.at[u], partner) for u in range(9)
     ]
-    aux_copy = remote(aux_own, aux_all.at[z, 1], aux_sems.at[0], aux_sems.at[1], partner)
+    aux_copy = remote(aux_own.at[0], aux_own.at[1], aux_sems.at[0], aux_sems.at[1], partner)
 
     for step, j in enumerate(ORDER):
         w_loads[j].wait()
         product = jnp.dot(lhs[...], w_v[j], preferred_element_type=F32)
-        aux_own[2 + j : 3 + j, :] = product[T : T + 1, :] + product[T + 1 : T + 2, :]
+        weights_sum = product[T : T + 1, :] + product[T + 1 : T + 2, :]
+        for o in range(6):
+            aux_own[0, o, j : j + 1, :] = weights_sum[:, (o // 2) * K : (o // 2 + 1) * K]
 
         @pl.when(active)
         def _():
@@ -103,13 +114,15 @@
             pl.semaphore_wait(barrier, 1 + (ZS - 1) + (COLS - 1))
 
         @pl.when(jnp.logical_not(active))
-        def _():
-            for h in range(3):
-                y_copies[3 * j + h].start()
-
-    @pl.when(jnp.logical_not(active))
-    def _():
-        aux_copy.start()
+        def _(step=step):
+            if step == 0:
+                for h in range(3):
+                    y_copies[3 * ORDER[0] + h].start()
+            if step == 2:
+                aux_copy.start()
+                for later in ORDER[1:]:
+                    for h in range(3):
+                        y_copies[3 * later + h].start()
 
     def z_copy(u, o):
         return remote(
@@ -117,17 +130,10 @@
         )
 
     def aux_z_copy(o):
-        return remote(aux_all.at[z], aux_all.at[z], auxz_send.at[o], auxz_recv.at[z], at_z(owner_z(o)))
+        return remote(aux_own.at[:, o], aux_all.at[z], auxz_send.at[o], auxz_recv.at[z], at_z(owner_z(o)))
 
     @pl.when(active)
     def _():
-        aux_all[z, 0] = aux_own[...]
-        aux_copy.wait_recv()
-        for o in range(6):
-            @pl.when(z != owner_z(o))
-            def _(o=o):
-                aux_z_copy(o).start()
-
         for j in ORDER:
             for h in range(3):
                 u = 3 * j + h
@@ -146,8 +152,19 @@
                     def _(j=j, total=total):
                         acc[j] = total
 
+            if j == ORDER[0]:
+                aux_copy.wait_recv()
+                for o in range(6):
+                    @pl.when(z != owner_z(o))
+                    def _(o=o):
+                        aux_z_copy(o).start()
+
+                    @pl.when(z == owner_z(o))
+                    def _(o=o):
+                        aux_all[z] = aux_own[:, o]
+
     kv_copy = remote(
-        qkv.at[pl.ds(1, 2), half], qkv.at[pl.ds(1, 2), half], kv_send.at[0], kv_recv.at[0], at_z(z + 1 - 2 * half)
+        qkv.at[pl.ds(1, 2), half], qkv.at[pl.ds(1, 2), half], kv_send.at[0], kv_recv.at[0], at_z(owner_z(mine + 1 - 2 * half))
     )
 
     def at_copy(o, d):
@@ -161,30 +178,29 @@
         for d in range(1, ZS):
             other = (z + d) % ZS
             remote(
-                aux_all.at[other], aux_all.at[other], auxz_send.at[0], auxz_recv.at[other], at_z(other)
+              aux_all.at[other], aux_all.at[other], auxz_send.at[0], auxz_recv.at[other], at_z(other)
             ).wait_recv()
-        flat = aux_all[...].reshape(2 * ZS, 8, T)
-        means = flat[:, 0, :]
+        def gathered(r):
+            return aux_all[:, :, r, :].reshape(2 * ZS, K)
+
+        means = jnp.concatenate([gathered(3), gathered(4)], axis=1)
         average = jnp.sum(means, axis=0, keepdims=True) * (1.0 / 16)
         offsets = means - average
-        spread = jnp.sum(flat[:, 1, :] + T * (offsets * offsets), axis=0, keepdims=True) * (1.0 / FEATURES)
+        sums = jnp.concatenate([gathered(5), gathered(6)], axis=1)
+        spread = jnp.sum(sums + T * (offsets * offsets), axis=0, keepdims=True) * (1.0 / FEATURES)
         scale = lax.rsqrt(spread + EPSILON)
-        stacked = jnp.concatenate([offsets, jnp.broadcast_to(scale, (112, T))], axis=0)
-        tall[...] = stacked.T
-        tall_half = tall[pl.ds(pl.multiple_of(half * HALF, HALF), HALF), :]
-        scale_col = tall_half[:, 16:17]
-        offset_cols = tall_half[:, 0:16]
-        lane0 = pl.multiple_of(head * K, K)
+        tall = jnp.concatenate([offsets, jnp.broadcast_to(scale, (112, 2 * K))], axis=0).T
+        scale_col = tall[0:HALF, 16:17]
+        offset_cols = tall[0:HALF, 0:16]
 
         for j in ORDER:
-            weights_sum = aux_all[:, :, 2 + j, pl.ds(lane0, K)].reshape(2 * ZS, K)
             total = acc[j] + jnp.dot(
-                offset_cols, weights_sum, preferred_element_type=F32, precision=lax.Precision.HIGHEST
+                offset_cols, gathered(j), preferred_element_type=F32, precision=lax.Precision.HIGHEST
             )
             for d in range(1, ZS):
                 other = (z + d) % ZS
                 remote(
-                    z_in.at[other, j], z_in.at[other, j], z_send.at[0, 0], z_recv.at[other, j], at_z(other)
+                  z_in.at[other, j], z_in.at[other, j], z_send.at[0, 0], z_recv.at[other, j], at_z(other)
                 ).wait_recv()
                 total = total + z_in[other, j].astype(F32)
             qkv[j, half] = (total * scale_col).astype(BF16)
@@ -288,32 +304,32 @@
     dma = pltpu.SemaphoreType.DMA
     return pl.pallas_call(
         kernel,
-        out_shape=jax.ShapeDtypeStruct((T, T), BF16),
+        out_shape=pltpu.VMEM((T, T), BF16),
         in_specs=[
             pl.BlockSpec(memory_space=pl.ANY),
-            pl.BlockSpec(memory_space=pltpu.VMEM),
+            pl.BlockSpec(memory_space=pl.ANY),
             pl.BlockSpec(memory_space=pl.ANY),
             pl.BlockSpec(memory_space=pl.ANY),
         ],
         out_specs=pl.BlockSpec(memory_space=pltpu.VMEM),
         scratch_shapes=[
             pltpu.VMEM((T, T), BF16),
+            pltpu.VMEM((T,), F32),
             pltpu.VMEM((3, T, T), BF16),
             pltpu.VMEM((T, T), BF16),
             pltpu.VMEM((T + 16, T), BF16),
-            pltpu.VMEM((8, T), F32),
-            pltpu.VMEM((ZS, 2, 8, T), F32),
+            pltpu.VMEM((2, 6, 8, K), F32),
+            pltpu.VMEM((ZS, 2, 8, K), F32),
             pltpu.VMEM((9, T, K), F32),
             pltpu.VMEM((9, T, K), BF16),
             pltpu.VMEM((9, 2, HALF, K), BF16),
             pltpu.VMEM((ZS, 3, HALF, K), BF16),
             pltpu.VMEM((3, HALF, K), F32),
             pltpu.VMEM((3, 2, HALF, K), BF16),
-            pltpu.VMEM((T, 128), F32),
             pltpu.VMEM((6, HALF, K), BF16),
             pltpu.VMEM((COLS, BLOCK, T), BF16),
             pltpu.VMEM((COLS, BLOCK, T), BF16),
-            dma((5,)),
+            dma((6,)),
             dma((2,)),
             dma((6,)),
             dma((ZS,)),

time: 68.7 us -> 60 us (0.87)
  Pallas kernels: 66.8 us -> 59.2 us
  local copies, waits for them, and re-layouts: 1.71 us -> 0.72 us
    pallas_call x1, Pallas kernels: 66.8 us -> 59.2 us  [shards(): pl.pallas_call(kernel, out_shape=pltpu.VMEM((T, T), BF16), in_specs=[pl.B...]
    unnamed x1, local copies, waits for them, and re-layouts: 1.71 us -> 0.72 us
where the time goes in v2:
time: 60 us; the launch traced here: 59.9 us
  Pallas kernels  59.2 us (99%)
  local copies, waits for them, and re-layouts  0.72 us (1%)
    pallas_call x1, Pallas kernels, shards(): pl.pallas_call(kernel, out_shape=pltpu.VMEM((T, T), BF16), in_specs=[pl.B...  59.2 us

profile of v2, /device:TPU:57, one launch (start us, length us, event | category | flops | bytes accessed | tf_op | source)
XLA Modules:
  0.0 59.9 jit_solution(14880184920270666205)
XLA Ops:
  0.0 59.2 %sublayer.1 = bf16[384,384]{1,0:T(8,128)(2,1)S(1)} custom-call(bf16[384,384]{1,0:T(8,128)(2,1)} %x_hbm.1, f32[384]{0:T(512)} %gain_hbm.1, bf16[3,384,384]{2,1,0:T(8,128)(2,1)} %bitcast.1, bf16[384,384]{1,0:T(8,128)(2,1)} %wo_hbm.1), custom_call_target="tpu_custom_call" | custom-call | tf_op jit(solution)/shard_map/sublayer/pallas_call | solution.py:305
  59.2 0.7 %copy.6 = bf16[384,384]{1,0:T(8,128)(2,1)} copy(bf16[384,384]{1,0:T(8,128)(2,1)S(1)} %sublayer.1) | data formatting | bytes 589824

commit v3 on v2

v3 whole, which is shorter than its diff:
```python
import math

import jax
import jax.numpy as jnp
from jax import lax
from jax.experimental import pallas as pl
from jax.experimental.pallas import tpu as pltpu
from jax.sharding import PartitionSpec as P

K = 128
EPSILON = 1e-05
F32 = jnp.float32
BF16 = jnp.bfloat16
T = 384
HALF = 192
BLOCK = 48
ZS = 8
COLS = 8
FEATURES = 6144
ORDER = (1, 2, 0)
EARLY = 2
MESH = pl.DeviceIdType.MESH


def owner_z(owner):
    return owner + owner // 3


def kernel(
    x_hbm, gain_hbm, w_hbm, wo_hbm, o_ref,
    x_v, gain_v, w_v, wo_v, lhs, aux_own, aux_all, part, y_buf, z_buf, z_in, tie_in, acc, qkv, att, p_buf, p_in,
    load_sem, aux_sems, auxz_send, auxz_recv, y_send, y_recv, z_send, z_recv, tie_recv,
    kv_send, kv_recv, at_send, at_recv, ay_send, ay_recv, rs_send, rs_recv, ag_send, ag_recv,
):
    row = lax.axis_index("row")
    col = lax.axis_index("col")
    y = row // ZS
    z = row % ZS
    x = col // 2
    core = col % 2
    active = y == core
    partner = {"row": (1 - y) * ZS + z}
    is_owner = jnp.logical_and(active, z % 4 != 3)
    mine = z - z // 4
    head = mine // 2
    half = mine % 2

    def at_z(other):
        return {"row": y * ZS + other}

    def remote(src, dst, send, recv, device):
        return pltpu.make_async_remote_copy(
            src_ref=src, dst_ref=dst, send_sem=send, recv_sem=recv, device_id=device, device_id_type=MESH
        )

    x_load = pltpu.make_async_copy(x_hbm, x_v, load_sem.at[0])
    x_load.start()
    w_loads = [pltpu.make_async_copy(w_hbm.at[j], w_v.at[j], load_sem.at[1 + j]) for j in range(3)]
    for j in ORDER:
        w_loads[j].start()
    gain_load = pltpu.make_async_copy(gain_hbm, gain_v, load_sem.at[5])
    gain_load.start()
    wo_load = pltpu.make_async_copy(wo_hbm, wo_v, load_sem.at[4])
    wo_load.start()

    barrier = pltpu.get_barrier_semaphore()
    pl.semaphore_signal(barrier, inc=1, device_id=partner, device_id_type=MESH)
    for d in range(1, ZS):
        pl.semaphore_signal(barrier, inc=1, device_id=at_z((z + d) % ZS), device_id_type=MESH)
    for d in range(1, COLS):
        pl.semaphore_signal(barrier, inc=1, device_id={"col": (col + d) % COLS}, device_id_type=MESH)

    x_load.wait()
    values = x_v[...].astype(F32)
    mean = jnp.sum(values, axis=1, keepdims=True) * (1.0 / T)
    centered = values - mean
    squares = jnp.sum(centered * centered, axis=1, keepdims=True)
    gain_load.wait()
    gain = gain_v[...].reshape(1, T)
    lhs[0:T, :] = (centered * gain).astype(BF16)
    high = gain.astype(BF16).astype(F32)
    rows = lax.broadcasted_iota(jnp.int32, (16, T), 0)
    lhs[T : T + 16, :] = jnp.where(rows == 0, high, jnp.where(rows == 1, gain - high, 0.0)).astype(BF16)
    lanes = lax.broadcasted_iota(jnp.int32, (T, 128), 1)
    turned = jnp.where(lanes == 0, mean, jnp.where(lanes == 1, squares, 0.0)).T
    early = turned[0:8, :]
    late = pltpu.roll(early, T - HALF, 1)
    for o in range(6):
        source = early if o % 2 == 0 else late
        for r in range(2):
            aux_own[0, o, 3 + 2 * r : 4 + 2 * r, :] = source[r : r + 1, 0:K]
            aux_own[0, o, 4 + 2 * r : 5 + 2 * r, :] = source[r : r + 1, K : 2 * K]

    tie = (z + 4) % ZS
    first = jnp.where(tie % 4 == 3, (tie + 1) % ZS, tie)
    first = first - first // 4

    def order(i):
        return (first + i) % 6

    def y_copy(j, o):
        return remote(y_buf.at[j, o], y_buf.at[j, o], y_send.at[j, o], y_recv.at[j, o], partner)

    aux_copy = remote(aux_own.at[0], aux_own.at[1], aux_sems.at[0], aux_sems.at[1], partner)

    for step, j in enumerate(ORDER):
        w_loads[j].wait()
        product = jnp.dot(lhs[...], w_v[j], preferred_element_type=F32)
        weights_sum = product[T : T + 1, :] + product[T + 1 : T + 2, :]
        for o in range(6):
            aux_own[0, o, j : j + 1, :] = weights_sum[:, (o // 2) * K : (o // 2 + 1) * K]

        @pl.when(active)
        def _():
            for o in range(6):
                part[j, o] = product[(o % 2) * HALF : (o % 2 + 1) * HALF, (o // 2) * K : (o // 2 + 1) * K]

        @pl.when(jnp.logical_not(active))
        def _():
            for o in range(6):
                piece = product[(o % 2) * HALF : (o % 2 + 1) * HALF, (o // 2) * K : (o // 2 + 1) * K]
                y_buf[j, o] = piece.astype(BF16)

        if step == 0:
            pl.semaphore_wait(barrier, 1 + (ZS - 1) + (COLS - 1))

        @pl.when(jnp.logical_not(active))
        def _(step=step):
            if step == 0:
                for i in range(EARLY):
                    y_copy(ORDER[0], order(i)).start()
            if step == 2:
                aux_copy.start()
                for i in range(EARLY, 18):
                    y_copy(ORDER[i // 6], order(i % 6)).start()

    def z_copy(j, o, to):
        return remote(z_buf.at[j, o], z_in.at[z, j], z_send.at[j, o], z_recv.at[z, j], at_z(to))

    def tie_copy(j, o):
        return remote(z_buf.at[j, o], tie_in.at[j], z_send.at[j, o], tie_recv.at[j], at_z((z + 1) % ZS))

    def aux_z_copy(o):
        return remote(aux_own.at[:, o], aux_all.at[z], auxz_send.at[o], auxz_recv.at[z], at_z(owner_z(o)))

    @pl.when(active)
    def _():
        for i in range(18):
            j = ORDER[i // 6]
            o = order(i % 6)
            to = owner_z(o)
            ahead = (to - z + ZS) % ZS

            if i == EARLY:
                aux_copy.wait_recv()
                for owner in range(6):
                    @pl.when(z != owner_z(owner))
                    def _(owner=owner):
                        aux_z_copy(owner).start()

                    @pl.when(z == owner_z(owner))
                    def _(owner=owner):
                        aux_all[z] = aux_own[:, owner]

            y_copy(j, o).wait_recv()
            total = part[j, o] + y_buf[j, o].astype(F32)

            @pl.when(ahead == 0)
            def _(j=j, total=total):
                acc[j] = total

            @pl.when(ahead == 4)
            def _(j=j, o=o, total=total):
                z_buf[j, o] = total.astype(BF16)
                tie_copy(j, o).start()

            @pl.when(ahead == 3)
            def _(i=i, j=j, o=o, to=to, total=total):
                tie_copy(j, o).wait_recv()
                z_buf[j, o] = (total + tie_in[j].astype(F32)).astype(BF16)
                z_copy(j, o, to).start()

            @pl.when(jnp.logical_and(ahead != 0, jnp.logical_and(ahead != 3, ahead != 4)))
            def _(j=j, o=o, to=to, total=total):
                z_buf[j, o] = total.astype(BF16)
                z_copy(j, o, to).start()

    def kv_copy(j):
        return remote(
            qkv.at[j, half], qkv.at[j, half], kv_send.at[j - 1], kv_recv.at[j - 1], at_z(owner_z(mine + 1 - 2 * half))
        )

    def at_copy(o, d):
        return remote(att.at[o], att.at[o], at_send.at[d - 1], at_recv.at[o], at_z((z + d) % ZS))

    def at_forward(o):
        return remote(att.at[o], att.at[o], at_send.at[3], at_recv.at[o], at_z((z + 1) % ZS))

    def ay_copy(o):
        return remote(att.at[o], att.at[o], ay_send.at[o], ay_recv.at[o], partner)

    @pl.when(is_owner)
    def _():
        for d in range(1, ZS):
            other = (z + d) % ZS
            remote(aux_own.at[:, 0], aux_all.at[other], auxz_send.at[0], auxz_recv.at[other], at_z(other)).wait_recv()

        def gathered(r):
            return aux_all[:, :, r, :].reshape(2 * ZS, K)

        means = jnp.concatenate([gathered(3), gathered(4)], axis=1)
        average = jnp.sum(means, axis=0, keepdims=True) * (1.0 / 16)
        offsets = means - average
        sums = jnp.concatenate([gathered(5), gathered(6)], axis=1)
        spread = jnp.sum(sums + T * (offsets * offsets), axis=0, keepdims=True) * (1.0 / FEATURES)
        scale = lax.rsqrt(spread + EPSILON)
        tall = jnp.concatenate([offsets, jnp.broadcast_to(scale, (112, 2 * K))], axis=0).T
        scale_col = tall[0:HALF, 16:17]
        offset_cols = tall[0:HALF, 0:16]

        for j in ORDER:
            total = acc[j] + jnp.dot(
                offset_cols, gathered(j), preferred_element_type=F32, precision=lax.Precision.HIGHEST
            )
            for d in (1, 7, 2, 6, 5, 3):
                other = (z + ZS - d) % ZS
                remote(z_buf.at[j, 0], z_in.at[other, j], z_send.at[0, 0], z_recv.at[other, j], at_z(other)).wait_recv()
                total = total + z_in[other, j].astype(F32)
            qkv[j, half] = (total * scale_col).astype(BF16)
            if j > 0:
                kv_copy(j).start()

        kv_copy(1).wait_recv()
        queries = qkv[0, half]
        keys = qkv[1].reshape(T, K)
        scores = lax.dot_general(
            queries, keys, (((1,), (1,)), ((), ())), preferred_element_type=F32
        ) * (1.0 / math.sqrt(K))
        exponent = jnp.exp(scores - jnp.max(scores, axis=1, keepdims=True))
        weights = (exponent / jnp.sum(exponent, axis=1, keepdims=True)).astype(BF16)
        kv_copy(2).wait_recv()
        mixed = jnp.dot(weights, qkv[2].reshape(T, K), preferred_element_type=F32)
        att[mine] = mixed.astype(BF16)
        for d in (3, 5, 2, 6, 1, 7):
            at_copy(mine, d).start()

    def rs_copy(s, dx):
        there = (x + dx) % 4
        other = 2 * there + s
        return remote(p_buf.at[4 * s + there], p_in.at[col], rs_send.at[s, dx], rs_recv.at[col], {"col": other})

    def wait_load():
        wo_load.wait()

    for s in range(2):
        @pl.when(active)
        def _(s=s):
            for h in range(3):
                o = 2 * h + s

                @pl.when(z != owner_z(o))
                def _(o=o):
                    at_copy(o, 1).wait_recv()

                @pl.when(z == (owner_z(o) + 3) % ZS)
                def _(o=o):
                    at_forward(o).start()

                ay_copy(o).start()

        @pl.when(jnp.logical_not(active))
        def _(s=s):
            for h in range(3):
                ay_copy(2 * h + s).wait_recv()

        if s == 0:
            wait_load()
        attended = jnp.concatenate([att[2 * h + s] for h in range(3)], axis=1)
        product = jnp.dot(attended, wo_v[...], preferred_element_type=F32).astype(BF16)
        for b in range(4):
            p_buf[4 * s + b] = product[b * BLOCK : (b + 1) * BLOCK, :]
        for dx in (2, 1, 3):
            rs_copy(s, dx).start()

        @pl.when(core != s)
        def _(s=s):
            rs_copy(s, 0).start()

    def rows_of(other):
        start = (other % 2) * HALF + (other // 2) * BLOCK
        return o_ref.at[pl.ds(pl.multiple_of(start, BLOCK), BLOCK), :]

    def ag_copy(d):
        return remote(rows_of(col), rows_of(col), ag_send.at[d - 1], ag_recv.at[col], {"col": (col + d) % COLS})

    def from_peers():
        yield 2 * x + 1 - core
        for dx in (1, 3, 2):
            for k in range(2):
                yield 2 * ((x + dx) % 4) + k

    total = p_buf[4 * core + x].astype(F32)
    for n, other in enumerate(from_peers()):
        remote(p_buf.at[0], p_in.at[other], rs_send.at[0, 0], rs_recv.at[other], {"col": other}).wait_recv()
        total = total + p_in[other].astype(F32)
    rows_of(col)[...] = total.astype(BF16)
    for d in range(1, COLS):
        ag_copy(d).start()

    @pl.when(jnp.logical_not(active))
    def _():
        aux_copy.wait_send()
        for j in range(3):
            for o in range(6):
                y_copy(j, o).wait_send()

    @pl.when(active)
    def _():
        for o in range(6):
            ay_copy(o).wait_send()

            @pl.when(z == (owner_z(o) + 3) % ZS)
            def _(o=o):
                at_forward(o).wait_send()

            @pl.when(z != owner_z(o))
            def _(o=o):
                aux_z_copy(o).wait_send()
                for j in range(3):
                    z_copy(j, o, owner_z(o)).wait_send()

    @pl.when(is_owner)
    def _():
        kv_copy(1).wait_send()
        kv_copy(2).wait_send()
        for d in (3, 5, 2, 6, 1, 7):
            at_copy(mine, d).wait_send()

    for s in range(2):
        for dx in range(1, 4):
            rs_copy(s, dx).wait_send()

        @pl.when(core != s)
        def _(s=s):
            rs_copy(s, 0).wait_send()

    for n, other in enumerate(from_peers()):
        remote(rows_of(other), rows_of(other), ag_send.at[0], ag_recv.at[other], {"col": other}).wait_recv()
    for d in range(1, COLS):
        ag_copy(d).wait_send()


def shards(tokens, norm_gain, qkv_weight, out_weight):
    dma = pltpu.SemaphoreType.DMA
    return pl.pallas_call(
        kernel,
        out_shape=pltpu.VMEM((T, T), BF16),
        in_specs=[
            pl.BlockSpec(memory_space=pl.ANY),
            pl.BlockSpec(memory_space=pl.ANY),
            pl.BlockSpec(memory_space=pl.ANY),
            pl.BlockSpec(memory_space=pl.ANY),
        ],
        out_specs=pl.BlockSpec(memory_space=pltpu.VMEM),
        scratch_shapes=[
            pltpu.VMEM((T, T), BF16),
            pltpu.VMEM((T,), F32),
            pltpu.VMEM((3, T, T), BF16),
            pltpu.VMEM((T, T), BF16),
            pltpu.VMEM((T + 16, T), BF16),
            pltpu.VMEM((2, 6, 8, K), F32),
            pltpu.VMEM((ZS, 2, 8, K), F32),
            pltpu.VMEM((3, 6, HALF, K), F32),
            pltpu.VMEM((3, 6, HALF, K), BF16),
            pltpu.VMEM((3, 6, HALF, K), BF16),
            pltpu.VMEM((ZS, 3, HALF, K), BF16),
            pltpu.VMEM((3, HALF, K), BF16),
            pltpu.VMEM((3, HALF, K), F32),
            pltpu.VMEM((3, 2, HALF, K), BF16),
            pltpu.VMEM((6, HALF, K), BF16),
            pltpu.VMEM((COLS, BLOCK, T), BF16),
            pltpu.VMEM((COLS, BLOCK, T), BF16),
            dma((6,)),
            dma((2,)),
            dma((6,)),
            dma((ZS,)),
            dma((3, 6)),
            dma((3, 6)),
            dma((3, 6)),
            dma((ZS, 3)),
            dma((3,)),
            dma((2,)),
            dma((2,)),
            dma((ZS - 1,)),
            dma((6,)),
            dma((6,)),
            dma((6,)),
            dma((2, 4)),
            dma((COLS,)),
            dma((COLS - 1,)),
            dma((COLS,)),
        ],
        compiler_params=pltpu.CompilerParams(collective_id=0, has_side_effects=True),
        name="sublayer",
    )(tokens, norm_gain, jnp.transpose(qkv_weight, (1, 0, 2)), out_weight)


def solution(mesh):
    in_specs = (P("dp", "row"), P("row"), P("row", None, "col"), P("col", "row"))
    out_specs = P("dp", "row")
    return jax.shard_map(shards, mesh=mesh, in_specs=in_specs, out_specs=out_specs, check_vma=False)
```

time: 60 us -> 55.7 us (0.928)
  Pallas kernels: 59.2 us -> 54.5 us
    pallas_call x1, Pallas kernels: 59.2 us -> 54.5 us  [shards(): pl.pallas_call(kernel, out_shape=pltpu.VMEM((T, T), BF16), in_specs=[pl.B...]
where the time goes in v3:
time: 55.7 us; the launch traced here: 55.2 us
  Pallas kernels  54.5 us (98%)
  local copies, waits for them, and re-layouts  0.72 us (1%)
    pallas_call x1, Pallas kernels, shards(): pl.pallas_call(kernel, out_shape=pltpu.VMEM((T, T), BF16), in_specs=[pl.B...  54.5 us

profile of v3, /device:TPU:57, one launch (start us, length us, event | category | flops | bytes accessed | tf_op | source)
XLA Modules:
  0.0 55.2 jit_solution(6196752113891227672)
XLA Ops:
  0.0 54.5 %sublayer.1 = bf16[384,384]{1,0:T(8,128)(2,1)S(1)} custom-call(bf16[384,384]{1,0:T(8,128)(2,1)} %x_hbm.1, f32[384]{0:T(512)} %gain_hbm.1, bf16[3,384,384]{2,1,0:T(8,128)(2,1)} %bitcast.1, bf16[384,384]{1,0:T(8,128)(2,1)} %wo_hbm.1), custom_call_target="tpu_custom_call" | custom-call | tf_op jit(solution)/shard_map/sublayer/pallas_call | solution.py:355
  54.5 0.7 %copy.6 = bf16[384,384]{1,0:T(8,128)(2,1)} copy(bf16[384,384]{1,0:T(8,128)(2,1)S(1)} %sublayer.1) | data formatting | bytes 589824

commit v4 on v3

v4 whole, which is shorter than its diff:
```python
import math

import jax
import jax.numpy as jnp
from jax import lax
from jax.experimental import pallas as pl
from jax.experimental.pallas import tpu as pltpu
from jax.sharding import PartitionSpec as P

K = 128
EPSILON = 1e-05
F32 = jnp.float32
BF16 = jnp.bfloat16
T = 384
HALF = 192
BLOCK = 48
ZS = 8
XS = 4
FEATURES = 6144
ORDER = (2, 1, 0)
EARLY = 2
MESH = pl.DeviceIdType.MESH


def owner_z(owner):
    return owner + owner // 3


def kernel(
    x_hbm, gain_hbm, w_hbm, wo_hbm, o_ref,
    x_v, gain_v, w_v, wo_v, lhs, aux_own, aux_all, part, y_buf, z_buf, z_in, tie_in, acc, v_out, v_in, qkv, att,
    pair_out, pair_in, p_buf, p_in,
    load_sem, aux_sems, auxz_send, auxz_recv, y_send, y_recv, z_send, z_recv, tie_recv, v_sems,
    kv_send, kv_recv, at_send, at_recv, ay_send, ay_recv, pair_sems, rs_sems, ag_send, ag_recv,
):
    row = lax.axis_index("row")
    col = lax.axis_index("col")
    y = row // ZS
    z = row % ZS
    x = col // 2
    core = col % 2
    active = y == core
    partner = {"row": (1 - y) * ZS + z}
    pair = {"col": 2 * x + 1 - core}
    owns = z % 4 != 3
    is_owner = jnp.logical_and(active, owns)
    mine = z - z // 4
    head = mine // 2
    half = mine % 2

    def at_x(d):
        return {"col": 2 * ((x + d) % XS) + core}

    def at_z(other):
        return {"row": y * ZS + other}

    def remote(src, dst, send, recv, device):
        return pltpu.make_async_remote_copy(
            src_ref=src, dst_ref=dst, send_sem=send, recv_sem=recv, device_id=device, device_id_type=MESH
        )

    x_load = pltpu.make_async_copy(x_hbm, x_v, load_sem.at[0])
    x_load.start()
    w_loads = [pltpu.make_async_copy(w_hbm.at[j], w_v.at[j], load_sem.at[1 + j]) for j in range(3)]
    for j in ORDER:
        w_loads[j].start()
    gain_load = pltpu.make_async_copy(gain_hbm, gain_v, load_sem.at[5])
    gain_load.start()
    wo_load = pltpu.make_async_copy(wo_hbm, wo_v, load_sem.at[4])
    wo_load.start()

    barrier = pltpu.get_barrier_semaphore()
    pl.semaphore_signal(barrier, inc=1, device_id=partner, device_id_type=MESH)
    pl.semaphore_signal(barrier, inc=1, device_id=pair, device_id_type=MESH)
    for d in range(1, XS):
        pl.semaphore_signal(barrier, inc=1, device_id=at_x(d), device_id_type=MESH)
    pl.semaphore_signal(barrier, inc=1, device_id=at_z((z + 7) % ZS), device_id_type=MESH)

    @pl.when(owns)
    def _():
        for d in range(1, ZS - 1):
            pl.semaphore_signal(barrier, inc=1, device_id=at_z((z + d) % ZS), device_id_type=MESH)

    arrivals = 5 + jnp.where(owns, 5, 6) + jnp.where(z % 4 == 2, 1, 0)

    x_load.wait()
    values = x_v[...].astype(F32)
    mean = jnp.sum(values, axis=1, keepdims=True) * (1.0 / T)
    centered = values - mean
    squares = jnp.sum(centered * centered, axis=1, keepdims=True)
    gain_load.wait()
    gain = gain_v[...].reshape(1, T)
    lhs[0:T, :] = (centered * gain).astype(BF16)
    high = gain.astype(BF16).astype(F32)
    rows = lax.broadcasted_iota(jnp.int32, (16, T), 0)
    lhs[T : T + 16, :] = jnp.where(rows == 0, high, jnp.where(rows == 1, gain - high, 0.0)).astype(BF16)
    lanes = lax.broadcasted_iota(jnp.int32, (T, 128), 1)
    turned = jnp.where(lanes == 0, mean, jnp.where(lanes == 1, squares, 0.0)).T
    early = turned[0:8, :]
    late = pltpu.roll(early, T - HALF, 1)
    for o in range(6):
        source = early if o % 2 == 0 else late
        for r in range(2):
            aux_own[0, o, 3 + 2 * r : 4 + 2 * r, :] = source[r : r + 1, 0:K]
            aux_own[0, o, 4 + 2 * r : 5 + 2 * r, :] = source[r : r + 1, K : 2 * K]

    tie = (z + 4) % ZS
    first = jnp.where(tie % 4 == 3, (tie + 1) % ZS, tie)
    first = first - first // 4

    def order(i):
        return (first + i) % 6

    def y_copy(n, o):
        return remote(y_buf.at[n, o], y_buf.at[n, o], y_send.at[0], y_recv.at[n, o], partner)

    aux_copy = remote(aux_own.at[0], aux_own.at[1], aux_sems.at[0], aux_sems.at[1], partner)

    def z_copy(j, o, to):
        return remote(z_buf.at[j, o], z_in.at[z, j], z_send.at[0], z_recv.at[j], at_z(to))

    def tie_copy(j, o):
        return remote(z_buf.at[j, o], tie_in.at[j], z_send.at[0], tie_recv.at[j], at_z((z + 1) % ZS))

    def aux_z_copy(o):
        return remote(aux_own.at[:, o], aux_all.at[z], auxz_send.at[0], auxz_recv.at[0], at_z(owner_z(o)))

    def z_send_piece(j, o, total, with_tie):
        to = owner_z(o)
        ahead = (to - z + ZS) % ZS

        @pl.when(ahead == 0)
        def _():
            acc[j] = total

        @pl.when(ahead == 4)
        def _():
            z_buf[j, o] = total.astype(BF16)
            tie_copy(j, o).start()

        if with_tie:
            @pl.when(ahead == 3)
            def _():
                tie_copy(j, o).wait_recv()
                z_buf[j, o] = (total + tie_in[j].astype(F32)).astype(BF16)
                z_copy(j, o, to).start()

        @pl.when(jnp.logical_and(ahead != 0, jnp.logical_and(ahead != 3, ahead != 4)))
        def _():
            z_buf[j, o] = total.astype(BF16)
            z_copy(j, o, to).start()

    for step, j in enumerate(ORDER):
        w_loads[j].wait()
        product = jnp.dot(lhs[...], w_v[j], preferred_element_type=F32)
        weights_sum = product[T : T + 1, :] + product[T + 1 : T + 2, :]
        for o in range(6):
            aux_own[0, o, j : j + 1, :] = weights_sum[:, (o // 2) * K : (o // 2 + 1) * K]

        def piece(o):
            return product[(o % 2) * HALF : (o % 2 + 1) * HALF, (o // 2) * K : (o // 2 + 1) * K]

        if step == 0:
            for o in range(6):
                part[j, o] = piece(o)
            pl.semaphore_wait(barrier, arrivals)
            for i in range(6):
                o = order(i)
                z_send_piece(j, o, part[j, o], False)
        else:
            @pl.when(active)
            def _():
                for o in range(6):
                    part[j, o] = piece(o)

            @pl.when(jnp.logical_not(active))
            def _(step=step):
                for o in range(6):
                    y_buf[step - 1, o] = piece(o).astype(BF16)
                if step == 1:
                    for i in range(EARLY):
                        y_copy(0, order(i)).start()
                else:
                    aux_copy.start()
                    for i in range(EARLY, 12):
                        y_copy(i // 6, order(i % 6)).start()

    @pl.when(z % 4 != 0)
    def _():
        o = order(5)
        tie_copy(2, o).wait_recv()
        z_buf[2, o] = (part[2, o] + tie_in[2].astype(F32)).astype(BF16)
        z_copy(2, o, (z + 3) % ZS).start()

    @pl.when(active)
    def _():
        for i in range(12):
            n = i // 6
            j = ORDER[1 + n]
            o = order(i % 6)

            if i == EARLY:
                aux_copy.wait_recv()
                for owner in range(6):
                    @pl.when(z != owner_z(owner))
                    def _(owner=owner):
                        aux_z_copy(owner).start()

                    @pl.when(z == owner_z(owner))
                    def _(owner=owner):
                        aux_all[z] = aux_own[:, owner]

            y_copy(n, o).wait_recv()
            z_send_piece(j, o, part[j, o] + y_buf[n, o].astype(F32), True)

    def kv_copy(j):
        return remote(
            qkv.at[j, half], qkv.at[j, half], kv_send.at[j - 1], kv_recv.at[j - 1], at_z(owner_z(mine + 1 - 2 * half))
        )

    def at_copy(d):
        return remote(att.at[mine], att.at[mine], at_send.at[0], at_recv.at[mine], at_z((z + d) % ZS))

    def at_forward(o):
        return remote(att.at[o], att.at[o], at_send.at[1], at_recv.at[o], at_z((z + 1) % ZS))

    def ay_copy(o):
        return remote(att.at[o], att.at[o], ay_send.at[0], ay_recv.at[o], partner)

    v_copy = remote(v_out, v_in, v_sems.at[0], v_sems.at[1], partner)

    def summed(j, start):
        remote(z_in.at[pl.ds(0, 6), 0], z_in.at[pl.ds(0, 6), j], z_send.at[0], z_recv.at[j], partner).wait_recv()
        total = start
        for d in (1, 7, 2, 6, 5, 3):
            total = total + z_in[(z + ZS - d) % ZS, j].astype(F32)
        return total

    @pl.when(jnp.logical_and(jnp.logical_not(active), owns))
    def _():
        v_out[...] = summed(2, acc[2]).astype(BF16)
        v_copy.start()

    @pl.when(is_owner)
    def _():
        remote(
            aux_all.at[pl.ds(0, 7)], aux_all.at[pl.ds(0, 7)], auxz_send.at[0], auxz_recv.at[0], partner
        ).wait_recv()

        def gathered(r):
            return aux_all[:, :, r, :].reshape(2 * ZS, K)

        means = jnp.concatenate([gathered(3), gathered(4)], axis=1)
        average = jnp.sum(means, axis=0, keepdims=True) * (1.0 / 16)
        offsets = means - average
        sums = jnp.concatenate([gathered(5), gathered(6)], axis=1)
        spread = jnp.sum(sums + T * (offsets * offsets), axis=0, keepdims=True) * (1.0 / FEATURES)
        scale = lax.rsqrt(spread + EPSILON)
        tall = jnp.concatenate([offsets, jnp.broadcast_to(scale, (112, 2 * K))], axis=0).T
        scale_col = tall[0:HALF, 16:17]
        offset_cols = tall[0:HALF, 0:16]

        for j in ORDER:
            start = acc[j] + jnp.dot(
                offset_cols, gathered(j), preferred_element_type=F32, precision=lax.Precision.HIGHEST
            )
            if j == 2:
                v_copy.wait_recv()
                start = start + v_in[...].astype(F32)
            qkv[j, half] = (summed(j, start) * scale_col).astype(BF16)
            if j > 0:
                kv_copy(j).start()

        kv_copy(1).wait_recv()
        queries = qkv[0, half]
        keys = qkv[1].reshape(T, K)
        scores = lax.dot_general(
            queries, keys, (((1,), (1,)), ((), ())), preferred_element_type=F32
        ) * (1.0 / math.sqrt(K))
        exponent = jnp.exp(scores - jnp.max(scores, axis=1, keepdims=True))
        weights = (exponent / jnp.sum(exponent, axis=1, keepdims=True)).astype(BF16)
        kv_copy(2).wait_recv()
        mixed = jnp.dot(weights, qkv[2].reshape(T, K), preferred_element_type=F32)
        att[mine] = mixed.astype(BF16)
        for d in (3, 5, 2, 6, 1, 7):
            at_copy(d).start()

    pair_copy = remote(pair_out, pair_in, pair_sems.at[0], pair_sems.at[1], pair)

    def rs_copy(d):
        return remote(p_buf.at[(x + d) % XS], p_in.at[x], rs_sems.at[0], rs_sems.at[1], at_x(d))

    for n in range(2):
        s = jnp.where(n == 0, 1 - core, core)

        @pl.when(active)
        def _(s=s, n=n):
            for h in range(3):
                o = 2 * h + s

                @pl.when(z != owner_z(o))
                def _(o=o, h=h):
                    remote(att.at[o], att.at[o], at_send.at[0], at_recv.at[o], partner).wait_recv()

                @pl.when(z == (owner_z(o) + 3) % ZS)
                def _(o=o):
                    at_forward(o).start()

                ay_copy(o).start()

        @pl.when(jnp.logical_not(active))
        def _(s=s, n=n):
            for h in range(3):
                ay_copy(2 * h + s).wait_recv()

        if n == 0:
            wo_load.wait()
        attended = jnp.concatenate([att[2 * h + s] for h in range(3)], axis=1)
        product = jnp.dot(attended, wo_v[...], preferred_element_type=F32)
        if n == 0:
            pair_out[...] = product.astype(BF16)
            pair_copy.start()
        else:
            pair_copy.wait_recv()
            both = (product + pair_in[...].astype(F32)).astype(BF16)
            for b in range(XS):
                p_buf[b] = both[b * BLOCK : (b + 1) * BLOCK, :]
            for d in (2, 1, 3):
                rs_copy(d).start()

    def rows_of(k, b):
        return o_ref.at[pl.ds(pl.multiple_of(k * HALF + b * BLOCK, BLOCK), BLOCK), :]

    def ag_copy(b, n, device):
        rows = rows_of(core, b)
        return remote(rows, rows, ag_send.at[n], ag_recv.at[core, b], device)

    remote(p_in.at[pl.ds(0, 3)], p_in.at[pl.ds(0, 3)], rs_sems.at[0], rs_sems.at[1], pair).wait_recv()
    total = p_buf[x].astype(F32)
    for d in (1, 3, 2):
        total = total + p_in[(x + d) % XS].astype(F32)
    rows_of(core, x)[...] = total.astype(BF16)
    for d in (2, 1, 3):
        ag_copy(x, 0, at_x(d)).start()
    ag_copy(x, 1, pair).start()

    def sent(ref, sem):
        remote(ref, ref, sem, sem, pair).wait_send()

    @pl.when(jnp.logical_not(active))
    def _():
        aux_copy.wait_send()
        sent(y_buf, y_send.at[0])

        @pl.when(owns)
        def _():
            v_copy.wait_send()
            sent(z_buf.at[0, pl.ds(0, 5)], z_send.at[0])

        @pl.when(jnp.logical_not(owns))
        def _():
            sent(z_buf.at[0], z_send.at[0])

    @pl.when(active)
    def _():
        sent(att, ay_send.at[0])

        @pl.when(z % 4 != 2)
        def _():
            sent(att.at[0], at_send.at[1])

        @pl.when(owns)
        def _():
            sent(aux_all.at[pl.ds(0, 5)], auxz_send.at[0])
            sent(z_buf.at[:, pl.ds(0, 5)], z_send.at[0])
            kv_copy(1).wait_send()
            kv_copy(2).wait_send()
            sent(att, at_send.at[0])

        @pl.when(jnp.logical_not(owns))
        def _():
            sent(aux_all.at[pl.ds(0, 6)], auxz_send.at[0])
            sent(z_buf, z_send.at[0])

    pair_copy.wait_send()
    sent(p_in.at[pl.ds(0, 3)], rs_sems.at[0])

    for d in (1, 3, 2):
        b = (x + d) % XS
        ag_copy(b, 0, pair).wait_recv()
        ag_copy(b, 1, pair).start()
    for d in (0, 1, 3, 2):
        b = (x + d) % XS
        remote(rows_of(1 - core, b), rows_of(1 - core, b), ag_send.at[0], ag_recv.at[1 - core, b], pair).wait_recv()
    sent(o_ref.at[pl.ds(0, 3 * BLOCK), :], ag_send.at[0])
    sent(o_ref.at[pl.ds(0, 4 * BLOCK), :], ag_send.at[1])


def shards(tokens, norm_gain, qkv_weight, out_weight):
    dma = pltpu.SemaphoreType.DMA
    return pl.pallas_call(
        kernel,
        out_shape=pltpu.VMEM((T, T), BF16),
        in_specs=[
            pl.BlockSpec(memory_space=pl.ANY),
            pl.BlockSpec(memory_space=pl.ANY),
            pl.BlockSpec(memory_space=pl.ANY),
            pl.BlockSpec(memory_space=pl.ANY),
        ],
        out_specs=pl.BlockSpec(memory_space=pltpu.VMEM),
        scratch_shapes=[
            pltpu.VMEM((T, T), BF16),
            pltpu.VMEM((T,), F32),
            pltpu.VMEM((3, T, T), BF16),
            pltpu.VMEM((T, T), BF16),
            pltpu.VMEM((T + 16, T), BF16),
            pltpu.VMEM((2, 6, 8, K), F32),
            pltpu.VMEM((ZS, 2, 8, K), F32),
            pltpu.VMEM((3, 6, HALF, K), F32),
            pltpu.VMEM((2, 6, HALF, K), BF16),
            pltpu.VMEM((3, 6, HALF, K), BF16),
            pltpu.VMEM((ZS, 3, HALF, K), BF16),
            pltpu.VMEM((3, HALF, K), BF16),
            pltpu.VMEM((3, HALF, K), F32),
            pltpu.VMEM((HALF, K), BF16),
            pltpu.VMEM((HALF, K), BF16),
            pltpu.VMEM((3, 2, HALF, K), BF16),
            pltpu.VMEM((6, HALF, K), BF16),
            pltpu.VMEM((HALF, T), BF16),
            pltpu.VMEM((HALF, T), BF16),
            pltpu.VMEM((XS, BLOCK, T), BF16),
            pltpu.VMEM((XS, BLOCK, T), BF16),
            dma((6,)),
            dma((2,)),
            dma((1,)),
            dma((1,)),
            dma((1,)),
            dma((2, 6)),
            dma((1,)),
            dma((3,)),
            dma((3,)),
            dma((2,)),
            dma((2,)),
            dma((2,)),
            dma((2,)),
            dma((6,)),
            dma((1,)),
            dma((6,)),
            dma((2,)),
            dma((2,)),
            dma((2,)),
            dma((2, XS)),
        ],
        compiler_params=pltpu.CompilerParams(collective_id=0, has_side_effects=True),
        name="sublayer",
    )(tokens, norm_gain, jnp.transpose(qkv_weight, (1, 0, 2)), out_weight)


def solution(mesh):
    in_specs = (P("dp", "row"), P("row"), P("row", None, "col"), P("col", "row"))
    out_specs = P("dp", "row")
    return jax.shard_map(shards, mesh=mesh, in_specs=in_specs, out_specs=out_specs, check_vma=False)
```

time: 55.7 us -> 56.5 us (1.014)
  Pallas kernels: 54.5 us -> 55.4 us
    pallas_call x1, Pallas kernels: 54.5 us -> 55.4 us  [shards(): pl.pallas_call(kernel, out_shape=pltpu.VMEM((T, T), BF16), in_specs=[pl.B...]
where the time goes in v4:
time: 56.5 us; the launch traced here: 56.1 us
  Pallas kernels  55.4 us (98%)
  local copies, waits for them, and re-layouts  0.72 us (1%)
    pallas_call x1, Pallas kernels, shards(): pl.pallas_call(kernel, out_shape=pltpu.VMEM((T, T), BF16), in_specs=[pl.B...  55.4 us

profile of v4, /device:TPU:57, one launch (start us, length us, event | category | flops | bytes accessed | tf_op | source)
XLA Modules:
  0.0 56.1 jit_solution(10921089711038997852)
XLA Ops:
  0.0 55.4 %sublayer.1 = bf16[384,384]{1,0:T(8,128)(2,1)S(1)} custom-call(bf16[384,384]{1,0:T(8,128)(2,1)} %x_hbm.1, f32[384]{0:T(512)} %gain_hbm.1, bf16[3,384,384]{2,1,0:T(8,128)(2,1)} %bitcast.1, bf16[384,384]{1,0:T(8,128)(2,1)} %wo_hbm.1), custom_call_target="tpu_custom_call" | custom-call | tf_op jit(solution)/shard_map/sublayer/pallas_call | solution.py:401
  55.4 0.7 %copy.6 = bf16[384,384]{1,0:T(8,128)(2,1)} copy(bf16[384,384]{1,0:T(8,128)(2,1)S(1)} %sublayer.1) | data formatting | bytes 589824

commit v5 on v4

--- a/solution.py
+++ b/solution.py
@@ -18,7 +18,7 @@
 XS = 4
 FEATURES = 6144
 ORDER = (2, 1, 0)
-EARLY = 2
+CHAINS = ((4, 5, 6, 2, 1, 0), (4, 5, 3, 7, 1, 0), (4, 3, 6, 2, 7, 0), (5, 3, 6, 2, 7, 1))
 MESH = pl.DeviceIdType.MESH
 
 
@@ -28,9 +28,9 @@
 
 def kernel(
     x_hbm, gain_hbm, w_hbm, wo_hbm, o_ref,
-    x_v, gain_v, w_v, wo_v, lhs, aux_own, aux_all, part, y_buf, z_buf, z_in, tie_in, acc, v_out, v_in, qkv, att,
+    x_v, gain_v, w_v, wo_v, lhs, aux_own, aux_all, part, y_buf, z_buf, plus_in, minus_in, acc, v_out, v_in, qkv, att,
     pair_out, pair_in, p_buf, p_in,
-    load_sem, aux_sems, auxz_send, auxz_recv, y_send, y_recv, z_send, z_recv, tie_recv, v_sems,
+    load_sem, aux_sems, auxz_send, auxz_recv, y_send, y_recv, z_send, plus_recv, minus_recv, v_sems,
     kv_send, kv_recv, at_send, at_recv, ay_send, ay_recv, pair_sems, rs_sems, ag_send, ag_recv,
 ):
     row = lax.axis_index("row")
@@ -76,12 +76,14 @@
         pl.semaphore_signal(barrier, inc=1, device_id=at_x(d), device_id_type=MESH)
     pl.semaphore_signal(barrier, inc=1, device_id=at_z((z + 7) % ZS), device_id_type=MESH)
 
+    pl.semaphore_signal(barrier, inc=1, device_id=at_z((z + 1) % ZS), device_id_type=MESH)
+
     @pl.when(owns)
     def _():
-        for d in range(1, ZS - 1):
+        for d in range(2, ZS - 1):
             pl.semaphore_signal(barrier, inc=1, device_id=at_z((z + d) % ZS), device_id_type=MESH)
 
-    arrivals = 5 + jnp.where(owns, 5, 6) + jnp.where(z % 4 == 2, 1, 0)
+    arrivals = 5 + jnp.where(owns, 5, 6) + jnp.where(z % 2 == 0, 1, 0)
 
     x_load.wait()
     values = x_v[...].astype(F32)
@@ -104,51 +106,77 @@
             aux_own[0, o, 3 + 2 * r : 4 + 2 * r, :] = source[r : r + 1, 0:K]
             aux_own[0, o, 4 + 2 * r : 5 + 2 * r, :] = source[r : r + 1, K : 2 * K]
 
-    tie = (z + 4) % ZS
-    first = jnp.where(tie % 4 == 3, (tie + 1) % ZS, tie)
-    first = first - first // 4
+    kind = z % 4
+
+    def ahead_of(i):
+        steps = [chain[i] for chain in CHAINS]
+        return jnp.where(kind == 0, steps[0], jnp.where(kind == 1, steps[1], jnp.where(kind == 2, steps[2], steps[3])))
+
+    aheads = [ahead_of(i) for i in range(6)]
 
     def order(i):
-        return (first + i) % 6
+        to = (z + aheads[i]) % ZS
+        return to - to // 4
 
     def y_copy(n, o):
         return remote(y_buf.at[n, o], y_buf.at[n, o], y_send.at[0], y_recv.at[n, o], partner)
 
     aux_copy = remote(aux_own.at[0], aux_own.at[1], aux_sems.at[0], aux_sems.at[1], partner)
 
-    def z_copy(j, o, to):
-        return remote(z_buf.at[j, o], z_in.at[z, j], z_send.at[0], z_recv.at[j], at_z(to))
-
-    def tie_copy(j, o):
-        return remote(z_buf.at[j, o], tie_in.at[j], z_send.at[0], tie_recv.at[j], at_z((z + 1) % ZS))
+    def plus_copy(j, o, ahead):
+        return remote(z_buf.at[j, o], plus_in.at[j, ahead - 1], z_send.at[0], plus_recv.at[j, ahead - 1], at_z((z + 1) % ZS))
+
+    def minus_copy(j, o, ahead):
+        return remote(z_buf.at[j, o], minus_in.at[j, 7 - ahead], z_send.at[0], minus_recv.at[j, 7 - ahead], at_z((z + 7) % ZS))
+
+    def plus_arrived(j, ahead):
+        remote(z_buf.at[j, 0], plus_in.at[j, ahead], z_send.at[0], plus_recv.at[j, ahead], partner).wait_recv()
+        return plus_in[j, ahead].astype(F32)
+
+    def minus_arrived(j, behind):
+        remote(z_buf.at[j, 0], minus_in.at[j, behind], z_send.at[0], minus_recv.at[j, behind], partner).wait_recv()
+        return minus_in[j, behind].astype(F32)
 
     def aux_z_copy(o):
         return remote(aux_own.at[:, o], aux_all.at[z], auxz_send.at[0], auxz_recv.at[0], at_z(owner_z(o)))
 
-    def z_send_piece(j, o, total, with_tie):
-        to = owner_z(o)
-        ahead = (to - z + ZS) % ZS
+    def z_step(j, i):
+        o = order(i)
+        ahead = aheads[i]
+
+        def term():
+            if j == 2:
+                return part[j, o]
+            return part[j, o] + y_buf[1 - j, o].astype(F32)
+
+        if j != 2:
+            y_copy(1 - j, o).wait_recv()
 
         @pl.when(ahead == 0)
         def _():
-            acc[j] = total
+            acc[j] = term()
 
         @pl.when(ahead == 4)
         def _():
-            z_buf[j, o] = total.astype(BF16)
-            tie_copy(j, o).start()
-
-        if with_tie:
-            @pl.when(ahead == 3)
-            def _():
-                tie_copy(j, o).wait_recv()
-                z_buf[j, o] = (total + tie_in[j].astype(F32)).astype(BF16)
-                z_copy(j, o, to).start()
-
-        @pl.when(jnp.logical_and(ahead != 0, jnp.logical_and(ahead != 3, ahead != 4)))
-        def _():
-            z_buf[j, o] = total.astype(BF16)
-            z_copy(j, o, to).start()
+            z_buf[j, o] = term().astype(BF16)
+            plus_copy(j, o, ahead).start()
+
+        @pl.when(ahead == 5)
+        def _():
+            z_buf[j, o] = term().astype(BF16)
+            minus_copy(j, o, ahead).start()
+
+        @pl.when(jnp.logical_and(ahead > 0, ahead < 4))
+        def _():
+            before = plus_arrived(j, ahead)
+            z_buf[j, o] = (before + term()).astype(BF16)
+            plus_copy(j, o, ahead).start()
+
+        @pl.when(ahead > 5)
+        def _():
+            before = minus_arrived(j, 8 - ahead)
+            z_buf[j, o] = (before + term()).astype(BF16)
+            minus_copy(j, o, ahead).start()
 
     for step, j in enumerate(ORDER):
         w_loads[j].wait()
@@ -164,9 +192,8 @@
             for o in range(6):
                 part[j, o] = piece(o)
             pl.semaphore_wait(barrier, arrivals)
-            for i in range(6):
-                o = order(i)
-                z_send_piece(j, o, part[j, o], False)
+            for i in range(2):
+                z_step(j, i)
         else:
             @pl.when(active)
             def _():
@@ -178,40 +205,36 @@
                 for o in range(6):
                     y_buf[step - 1, o] = piece(o).astype(BF16)
                 if step == 1:
-                    for i in range(EARLY):
-                        y_copy(0, order(i)).start()
+                    y_copy(0, order(0)).start()
                 else:
+                    y_copy(1, order(0)).start()
                     aux_copy.start()
-                    for i in range(EARLY, 12):
-                        y_copy(i // 6, order(i % 6)).start()
-
-    @pl.when(z % 4 != 0)
-    def _():
-        o = order(5)
-        tie_copy(2, o).wait_recv()
-        z_buf[2, o] = (part[2, o] + tie_in[2].astype(F32)).astype(BF16)
-        z_copy(2, o, (z + 3) % ZS).start()
+                    for i in range(1, 6):
+                        for n in range(2):
+                            y_copy(n, order(i)).start()
+
+    @pl.when(jnp.logical_not(active))
+    def _():
+        for i in range(2, 6):
+            z_step(2, i)
 
     @pl.when(active)
     def _():
-        for i in range(12):
-            n = i // 6
-            j = ORDER[1 + n]
-            o = order(i % 6)
-
-            if i == EARLY:
-                aux_copy.wait_recv()
-                for owner in range(6):
-                    @pl.when(z != owner_z(owner))
-                    def _(owner=owner):
-                        aux_z_copy(owner).start()
-
-                    @pl.when(z == owner_z(owner))
-                    def _(owner=owner):
-                        aux_all[z] = aux_own[:, owner]
-
-            y_copy(n, o).wait_recv()
-            z_send_piece(j, o, part[j, o] + y_buf[n, o].astype(F32), True)
+        z_step(2, 2)
+        z_step(1, 0)
+        z_step(0, 0)
+        aux_copy.wait_recv()
+        for owner in range(6):
+            @pl.when(z != owner_z(owner))
+            def _(owner=owner):
+                aux_z_copy(owner).start()
+
+            @pl.when(z == owner_z(owner))
+            def _(owner=owner):
+                aux_all[z] = aux_own[:, owner]
+
+        for j, i in ((1, 1), (0, 1), (2, 3), (1, 2), (0, 2), (2, 4), (1, 3), (0, 3), (2, 5), (1, 4), (0, 4), (1, 5), (0, 5)):
+            z_step(j, i)
 
     def kv_copy(j):
         return remote(
@@ -230,10 +253,8 @@
     v_copy = remote(v_out, v_in, v_sems.at[0], v_sems.at[1], partner)
 
     def summed(j, start):
-        remote(z_in.at[pl.ds(0, 6), 0], z_in.at[pl.ds(0, 6), j], z_send.at[0], z_recv.at[j], partner).wait_recv()
-        total = start
-        for d in (1, 7, 2, 6, 5, 3):
-            total = total + z_in[(z + ZS - d) % ZS, j].astype(F32)
+        total = start + plus_arrived(j, 0)
+        total = total + minus_arrived(j, 0)
         return total
 
     @pl.when(jnp.logical_and(jnp.logical_not(active), owns))
@@ -419,8 +440,8 @@
             pltpu.VMEM((3, 6, HALF, K), F32),
             pltpu.VMEM((2, 6, HALF, K), BF16),
             pltpu.VMEM((3, 6, HALF, K), BF16),
-            pltpu.VMEM((ZS, 3, HALF, K), BF16),
-            pltpu.VMEM((3, HALF, K), BF16),
+            pltpu.VMEM((3, 4, HALF, K), BF16),
+            pltpu.VMEM((3, 3, HALF, K), BF16),
             pltpu.VMEM((3, HALF, K), F32),
             pltpu.VMEM((HALF, K), BF16),
             pltpu.VMEM((HALF, K), BF16),
@@ -437,8 +458,8 @@
             dma((1,)),
             dma((2, 6)),
             dma((1,)),
-            dma((3,)),
-            dma((3,)),
+            dma((3, 4)),
+            dma((3, 3)),
             dma((2,)),
             dma((2,)),
             dma((2,)),

time: 56.5 us -> 60.4 us (1.069)
  Pallas kernels: 55.4 us -> 59.5 us
    pallas_call x1, Pallas kernels: 55.4 us -> 59.5 us  [shards(): pl.pallas_call(kernel, out_shape=pltpu.VMEM((T, T), BF16), in_specs=[pl.B...]
where the time goes in v5:
time: 60.4 us; the launch traced here: 60.2 us
  Pallas kernels  59.5 us (99%)
  local copies, waits for them, and re-layouts  0.72 us (1%)
    pallas_call x1, Pallas kernels, shards(): pl.pallas_call(kernel, out_shape=pltpu.VMEM((T, T), BF16), in_specs=[pl.B...  59.5 us

profile of v5, /device:TPU:57, one launch (start us, length us, event | category | flops | bytes accessed | tf_op | source)
XLA Modules:
  0.0 60.2 jit_solution(6137613041656336414)
XLA Ops:
  0.0 59.5 %sublayer.1 = bf16[384,384]{1,0:T(8,128)(2,1)S(1)} custom-call(bf16[384,384]{1,0:T(8,128)(2,1)} %x_hbm.1, f32[384]{0:T(512)} %gain_hbm.1, bf16[3,384,384]{2,1,0:T(8,128)(2,1)} %bitcast.1, bf16[384,384]{1,0:T(8,128)(2,1)} %wo_hbm.1), custom_call_target="tpu_custom_call" | custom-call | tf_op jit(solution)/shard_map/sublayer/pallas_call | solution.py:422
  59.5 0.7 %copy.6 = bf16[384,384]{1,0:T(8,128)(2,1)} copy(bf16[384,384]{1,0:T(8,128)(2,1)S(1)} %sublayer.1) | data formatting | bytes 589824

commit v6 on v4

--- a/solution.py
+++ b/solution.py
@@ -17,7 +17,7 @@
 ZS = 8
 XS = 4
 FEATURES = 6144
-ORDER = (2, 1, 0)
+ORDER = (1, 2, 0)
 EARLY = 2
 MESH = pl.DeviceIdType.MESH
 
@@ -28,9 +28,9 @@
 
 def kernel(
     x_hbm, gain_hbm, w_hbm, wo_hbm, o_ref,
-    x_v, gain_v, w_v, wo_v, lhs, aux_own, aux_all, part, y_buf, z_buf, z_in, tie_in, acc, v_out, v_in, qkv, att,
+    x_v, gain_v, w_v, wo_v, lhs, aux_own, aux_all, part, y_buf, z_buf, z_in, tie_in, acc, qkv, att,
     pair_out, pair_in, p_buf, p_in,
-    load_sem, aux_sems, auxz_send, auxz_recv, y_send, y_recv, z_send, z_recv, tie_recv, v_sems,
+    load_sem, aux_sems, auxz_send, auxz_recv, y_send, y_recv, z_send, z_recv, tie_recv,
     kv_send, kv_recv, at_send, at_recv, ay_send, ay_recv, pair_sems, rs_sems, ag_send, ag_recv,
 ):
     row = lax.axis_index("row")
@@ -74,14 +74,16 @@
     pl.semaphore_signal(barrier, inc=1, device_id=pair, device_id_type=MESH)
     for d in range(1, XS):
         pl.semaphore_signal(barrier, inc=1, device_id=at_x(d), device_id_type=MESH)
-    pl.semaphore_signal(barrier, inc=1, device_id=at_z((z + 7) % ZS), device_id_type=MESH)
-
-    @pl.when(owns)
+    @pl.when(active)
+    def _():
+        pl.semaphore_signal(barrier, inc=1, device_id=at_z((z + 7) % ZS), device_id_type=MESH)
+
+    @pl.when(is_owner)
     def _():
         for d in range(1, ZS - 1):
             pl.semaphore_signal(barrier, inc=1, device_id=at_z((z + d) % ZS), device_id_type=MESH)
 
-    arrivals = 5 + jnp.where(owns, 5, 6) + jnp.where(z % 4 == 2, 1, 0)
+    arrivals = 5 + jnp.where(active, jnp.where(owns, 5, 6) + jnp.where(z % 4 == 2, 1, 0), 0)
 
     x_load.wait()
     values = x_v[...].astype(F32)
@@ -125,31 +127,6 @@
     def aux_z_copy(o):
         return remote(aux_own.at[:, o], aux_all.at[z], auxz_send.at[0], auxz_recv.at[0], at_z(owner_z(o)))
 
-    def z_send_piece(j, o, total, with_tie):
-        to = owner_z(o)
-        ahead = (to - z + ZS) % ZS
-
-        @pl.when(ahead == 0)
-        def _():
-            acc[j] = total
-
-        @pl.when(ahead == 4)
-        def _():
-            z_buf[j, o] = total.astype(BF16)
-            tie_copy(j, o).start()
-
-        if with_tie:
-            @pl.when(ahead == 3)
-            def _():
-                tie_copy(j, o).wait_recv()
-                z_buf[j, o] = (total + tie_in[j].astype(F32)).astype(BF16)
-                z_copy(j, o, to).start()
-
-        @pl.when(jnp.logical_and(ahead != 0, jnp.logical_and(ahead != 3, ahead != 4)))
-        def _():
-            z_buf[j, o] = total.astype(BF16)
-            z_copy(j, o, to).start()
-
     for step, j in enumerate(ORDER):
         w_loads[j].wait()
         product = jnp.dot(lhs[...], w_v[j], preferred_element_type=F32)
@@ -160,44 +137,36 @@
         def piece(o):
             return product[(o % 2) * HALF : (o % 2 + 1) * HALF, (o // 2) * K : (o // 2 + 1) * K]
 
-        if step == 0:
+        @pl.when(active)
+        def _():
             for o in range(6):
                 part[j, o] = piece(o)
+
+        @pl.when(jnp.logical_not(active))
+        def _():
+            for o in range(6):
+                y_buf[j, o] = piece(o).astype(BF16)
+
+        if step == 0:
             pl.semaphore_wait(barrier, arrivals)
-            for i in range(6):
-                o = order(i)
-                z_send_piece(j, o, part[j, o], False)
-        else:
-            @pl.when(active)
-            def _():
-                for o in range(6):
-                    part[j, o] = piece(o)
-
-            @pl.when(jnp.logical_not(active))
-            def _(step=step):
-                for o in range(6):
-                    y_buf[step - 1, o] = piece(o).astype(BF16)
-                if step == 1:
-                    for i in range(EARLY):
-                        y_copy(0, order(i)).start()
-                else:
-                    aux_copy.start()
-                    for i in range(EARLY, 12):
-                        y_copy(i // 6, order(i % 6)).start()
-
-    @pl.when(z % 4 != 0)
-    def _():
-        o = order(5)
-        tie_copy(2, o).wait_recv()
-        z_buf[2, o] = (part[2, o] + tie_in[2].astype(F32)).astype(BF16)
-        z_copy(2, o, (z + 3) % ZS).start()
+
+        @pl.when(jnp.logical_not(active))
+        def _(step=step):
+            if step == 0:
+                for i in range(EARLY):
+                    y_copy(ORDER[0], order(i)).start()
+            if step == 2:
+                aux_copy.start()
+                for i in range(EARLY, 18):
+                    y_copy(ORDER[i // 6], order(i % 6)).start()
 
     @pl.when(active)
     def _():
-        for i in range(12):
-            n = i // 6
-            j = ORDER[1 + n]
+        for i in range(18):
+            j = ORDER[i // 6]
             o = order(i % 6)
+            to = owner_z(o)
+            ahead = (to - z + ZS) % ZS
 
             if i == EARLY:
                 aux_copy.wait_recv()
@@ -210,8 +179,28 @@
                     def _(owner=owner):
                         aux_all[z] = aux_own[:, owner]
 
-            y_copy(n, o).wait_recv()
-            z_send_piece(j, o, part[j, o] + y_buf[n, o].astype(F32), True)
+            y_copy(j, o).wait_recv()
+            total = part[j, o] + y_buf[j, o].astype(F32)
+
+            @pl.when(ahead == 0)
+            def _(j=j, total=total):
+                acc[j] = total
+
+            @pl.when(ahead == 4)
+            def _(j=j, o=o, total=total):
+                z_buf[j, o] = total.astype(BF16)
+                tie_copy(j, o).start()
+
+            @pl.when(ahead == 3)
+            def _(i=i, j=j, o=o, to=to, total=total):
+                tie_copy(j, o).wait_recv()
+                z_buf[j, o] = (total + tie_in[j].astype(F32)).astype(BF16)
+                z_copy(j, o, to).start()
+
+            @pl.when(jnp.logical_and(ahead != 0, jnp.logical_and(ahead != 3, ahead != 4)))
+            def _(j=j, o=o, to=to, total=total):
+                z_buf[j, o] = total.astype(BF16)
+                z_copy(j, o, to).start()
 
     def kv_copy(j):
         return remote(
@@ -226,8 +215,6 @@
 
     def ay_copy(o):
         return remote(att.at[o], att.at[o], ay_send.at[0], ay_recv.at[o], partner)
-
-    v_copy = remote(v_out, v_in, v_sems.at[0], v_sems.at[1], partner)
 
     def summed(j, start):
         remote(z_in.at[pl.ds(0, 6), 0], z_in.at[pl.ds(0, 6), j], z_send.at[0], z_recv.at[j], partner).wait_recv()
@@ -235,11 +222,6 @@
         for d in (1, 7, 2, 6, 5, 3):
             total = total + z_in[(z + ZS - d) % ZS, j].astype(F32)
         return total
-
-    @pl.when(jnp.logical_and(jnp.logical_not(active), owns))
-    def _():
-        v_out[...] = summed(2, acc[2]).astype(BF16)
-        v_copy.start()
 
     @pl.when(is_owner)
     def _():
@@ -264,9 +246,6 @@
             start = acc[j] + jnp.dot(
                 offset_cols, gathered(j), preferred_element_type=F32, precision=lax.Precision.HIGHEST
             )
-            if j == 2:
-                v_copy.wait_recv()
-                start = start + v_in[...].astype(F32)
             qkv[j, half] = (summed(j, start) * scale_col).astype(BF16)
             if j > 0:
                 kv_copy(j).start()
@@ -351,15 +330,6 @@
     def _():
         aux_copy.wait_send()
         sent(y_buf, y_send.at[0])
-
-        @pl.when(owns)
-        def _():
-            v_copy.wait_send()
-            sent(z_buf.at[0, pl.ds(0, 5)], z_send.at[0])
-
-        @pl.when(jnp.logical_not(owns))
-        def _():
-            sent(z_buf.at[0], z_send.at[0])
 
     @pl.when(active)
     def _():
@@ -417,13 +387,11 @@
             pltpu.VMEM((2, 6, 8, K), F32),
             pltpu.VMEM((ZS, 2, 8, K), F32),
             pltpu.VMEM((3, 6, HALF, K), F32),
-            pltpu.VMEM((2, 6, HALF, K), BF16),
+            pltpu.VMEM((3, 6, HALF, K), BF16),
             pltpu.VMEM((3, 6, HALF, K), BF16),
             pltpu.VMEM((ZS, 3, HALF, K), BF16),
             pltpu.VMEM((3, HALF, K), BF16),
             pltpu.VMEM((3, HALF, K), F32),
-            pltpu.VMEM((HALF, K), BF16),
-            pltpu.VMEM((HALF, K), BF16),
             pltpu.VMEM((3, 2, HALF, K), BF16),
             pltpu.VMEM((6, HALF, K), BF16),
             pltpu.VMEM((HALF, T), BF16),
@@ -435,11 +403,10 @@
             dma((1,)),
             dma((1,)),
             dma((1,)),
-            dma((2, 6)),
+            dma((3, 6)),
             dma((1,)),
             dma((3,)),
             dma((3,)),
-            dma((2,)),
             dma((2,)),
             dma((2,)),
             dma((2,)),

time: 56.5 us -> 56.1 us (level)
  no operation moved by 1% of the time
where the time goes in v6:
time: 56.1 us; the launch traced here: 56 us
  Pallas kernels  55.3 us (99%)
  local copies, waits for them, and re-layouts  0.72 us (1%)
    pallas_call x1, Pallas kernels, shards(): pl.pallas_call(kernel, out_shape=pltpu.VMEM((T, T), BF16), in_specs=[pl.B...  55.3 us

profile of v6, /device:TPU:57, one launch (start us, length us, event | category | flops | bytes accessed | tf_op | source)
XLA Modules:
  0.0 56.0 jit_solution(4478444208187008351)
XLA Ops:
  0.0 55.3 %sublayer.1 = bf16[384,384]{1,0:T(8,128)(2,1)S(1)} custom-call(bf16[384,384]{1,0:T(8,128)(2,1)} %x_hbm.1, f32[384]{0:T(512)} %gain_hbm.1, bf16[3,384,384]{2,1,0:T(8,128)(2,1)} %bitcast.1, bf16[384,384]{1,0:T(8,128)(2,1)} %wo_hbm.1), custom_call_target="tpu_custom_call" | custom-call | tf_op jit(solution)/shard_map/sublayer/pallas_call | solution.py:371
  55.3 0.7 %copy.6 = bf16[384,384]{1,0:T(8,128)(2,1)} copy(bf16[384,384]{1,0:T(8,128)(2,1)S(1)} %sublayer.1) | data formatting | bytes 589824

commit v7 on v6

--- a/solution.py
+++ b/solution.py
@@ -19,6 +19,7 @@
 FEATURES = 6144
 ORDER = (1, 2, 0)
 EARLY = 2
+NEAREST = ((0, 1, 2, 6, 5, 4), (0, 1, 7, 3, 5, 4), (0, 7, 2, 6, 3, 4), (1, 7, 2, 6, 3, 5))
 MESH = pl.DeviceIdType.MESH
 
 
@@ -29,7 +30,7 @@
 def kernel(
     x_hbm, gain_hbm, w_hbm, wo_hbm, o_ref,
     x_v, gain_v, w_v, wo_v, lhs, aux_own, aux_all, part, y_buf, z_buf, z_in, tie_in, acc, qkv, att,
-    pair_out, pair_in, p_buf, p_in,
+    out_acc, pair_out, pair_in, p_buf, p_in,
     load_sem, aux_sems, auxz_send, auxz_recv, y_send, y_recv, z_send, z_recv, tie_recv,
     kv_send, kv_recv, at_send, at_recv, ay_send, ay_recv, pair_sems, rs_sems, ag_send, ag_recv,
 ):
@@ -208,10 +209,7 @@
         )
 
     def at_copy(d):
-        return remote(att.at[mine], att.at[mine], at_send.at[0], at_recv.at[mine], at_z((z + d) % ZS))
-
-    def at_forward(o):
-        return remote(att.at[o], att.at[o], at_send.at[1], at_recv.at[o], at_z((z + 1) % ZS))
+        return remote(att.at[mine], att.at[mine], at_send.at[int(d == 4)], at_recv.at[mine], at_z((z + d) % ZS))
 
     def ay_copy(o):
         return remote(att.at[o], att.at[o], ay_send.at[0], ay_recv.at[o], partner)
@@ -261,7 +259,7 @@
         kv_copy(2).wait_recv()
         mixed = jnp.dot(weights, qkv[2].reshape(T, K), preferred_element_type=F32)
         att[mine] = mixed.astype(BF16)
-        for d in (3, 5, 2, 6, 1, 7):
+        for d in (4, 3, 5, 2, 6, 1, 7):
             at_copy(d).start()
 
     pair_copy = remote(pair_out, pair_in, pair_sems.at[0], pair_sems.at[1], pair)
@@ -269,43 +267,39 @@
     def rs_copy(d):
         return remote(p_buf.at[(x + d) % XS], p_in.at[x], rs_sems.at[0], rs_sems.at[1], at_x(d))
 
-    for n in range(2):
-        s = jnp.where(n == 0, 1 - core, core)
+    out_acc[...] = jnp.zeros_like(out_acc)
+    wo_load.wait()
+    kind = z % 4
+    for i in range(6):
+        near = [table[i] for table in NEAREST]
+        there = jnp.where(kind == 0, near[0], jnp.where(kind == 1, near[1], jnp.where(kind == 2, near[2], near[3])))
+        source = (z + there) % ZS
+        o = source - source // 4
 
         @pl.when(active)
-        def _(s=s, n=n):
-            for h in range(3):
-                o = 2 * h + s
-
-                @pl.when(z != owner_z(o))
-                def _(o=o, h=h):
-                    remote(att.at[o], att.at[o], at_send.at[0], at_recv.at[o], partner).wait_recv()
-
-                @pl.when(z == (owner_z(o) + 3) % ZS)
-                def _(o=o):
-                    at_forward(o).start()
-
-                ay_copy(o).start()
+        def _(o=o, i=i, there=there):
+            @pl.when(there != 0)
+            def _():
+                remote(att.at[o], att.at[o], at_send.at[0], at_recv.at[o], partner).wait_recv()
+
+            ay_copy(o).start()
 
         @pl.when(jnp.logical_not(active))
-        def _(s=s, n=n):
-            for h in range(3):
-                ay_copy(2 * h + s).wait_recv()
-
-        if n == 0:
-            wo_load.wait()
-        attended = jnp.concatenate([att[2 * h + s] for h in range(3)], axis=1)
-        product = jnp.dot(attended, wo_v[...], preferred_element_type=F32)
-        if n == 0:
-            pair_out[...] = product.astype(BF16)
-            pair_copy.start()
-        else:
-            pair_copy.wait_recv()
-            both = (product + pair_in[...].astype(F32)).astype(BF16)
-            for b in range(XS):
-                p_buf[b] = both[b * BLOCK : (b + 1) * BLOCK, :]
-            for d in (2, 1, 3):
-                rs_copy(d).start()
+        def _(o=o, i=i):
+            ay_copy(o).wait_recv()
+
+        weights = wo_v[pl.ds(pl.multiple_of((o // 2) * K, K), K), :]
+        out_acc[o % 2] += jnp.dot(att[o], weights, preferred_element_type=F32)
+
+    pair_out[...] = out_acc[1 - core].astype(BF16)
+    pair_copy.start()
+    mine_f32 = out_acc[core]
+    pair_copy.wait_recv()
+    both = (mine_f32 + pair_in[...].astype(F32)).astype(BF16)
+    for b in range(XS):
+        p_buf[b] = both[b * BLOCK : (b + 1) * BLOCK, :]
+    for d in (2, 1, 3):
+        rs_copy(d).start()
 
     def rows_of(k, b):
         return o_ref.at[pl.ds(pl.multiple_of(k * HALF + b * BLOCK, BLOCK), BLOCK), :]
@@ -335,10 +329,6 @@
     def _():
         sent(att, ay_send.at[0])
 
-        @pl.when(z % 4 != 2)
-        def _():
-            sent(att.at[0], at_send.at[1])
-
         @pl.when(owns)
         def _():
             sent(aux_all.at[pl.ds(0, 5)], auxz_send.at[0])
@@ -346,6 +336,7 @@
             kv_copy(1).wait_send()
             kv_copy(2).wait_send()
             sent(att, at_send.at[0])
+            sent(att.at[0], at_send.at[1])
 
         @pl.when(jnp.logical_not(owns))
         def _():
@@ -394,6 +385,7 @@
             pltpu.VMEM((3, HALF, K), F32),
             pltpu.VMEM((3, 2, HALF, K), BF16),
             pltpu.VMEM((6, HALF, K), BF16),
+            pltpu.VMEM((2, HALF, T), F32),
             pltpu.VMEM((HALF, T), BF16),
             pltpu.VMEM((HALF, T), BF16),
             pltpu.VMEM((XS, BLOCK, T), BF16),

time: 56.1 us -> 53.3 us (0.950)
  Pallas kernels: 55.3 us -> 52.3 us
    pallas_call x1, Pallas kernels: 55.3 us -> 52.3 us  [shards(): pl.pallas_call(kernel, out_shape=pltpu.VMEM((T, T), BF16), in_specs=[pl.B...]
where the time goes in v7:
time: 53.3 us; the launch traced here: 53 us
  Pallas kernels  52.3 us (98%)
  local copies, waits for them, and re-layouts  0.72 us (1%)
    pallas_call x1, Pallas kernels, shards(): pl.pallas_call(kernel, out_shape=pltpu.VMEM((T, T), BF16), in_specs=[pl.B...  52.3 us

profile of v7, /device:TPU:57, one launch (start us, length us, event | category | flops | bytes accessed | tf_op | source)
XLA Modules:
  0.0 53.0 jit_solution(17757907070853852594)
XLA Ops:
  0.0 52.3 %sublayer.1 = bf16[384,384]{1,0:T(8,128)(2,1)S(1)} custom-call(bf16[384,384]{1,0:T(8,128)(2,1)} %x_hbm.1, f32[384]{0:T(512)} %gain_hbm.1, bf16[3,384,384]{2,1,0:T(8,128)(2,1)} %bitcast.1, bf16[384,384]{1,0:T(8,128)(2,1)} %wo_hbm.1), custom_call_target="tpu_custom_call" | custom-call | tf_op jit(solution)/shard_map/sublayer/pallas_call | solution.py:362
  52.3 0.7 %copy.6 = bf16[384,384]{1,0:T(8,128)(2,1)} copy(bf16[384,384]{1,0:T(8,128)(2,1)S(1)} %sublayer.1) | data formatting | bytes 589824
